TPU v7x, 768 devices: a whole 4x8x12 slice. The times are simulated.
768 devices in a mesh: dp: 12 (over z), mp: 64 (over x, y, core).
Axes of the slice: x: 4, y: 8, z: 12, core: 2. Of those that a mesh axis runs over, the one named last changes fastest.
Arguments:
- grad_parts: bfloat16 [12, 64, 2, 2304, 128], P('dp', 'mp'), may hold values from -45 to 45
- master: float32 [64, 2, 2304, 128], P('mp', None, 'dp'), may hold values from -15 to 15
- momenta: float32 [3, 64, 2, 2304, 128], P(None, 'mp', None, 'dp'), may hold values from -45 to 45
- second: float32 [3, 64, 2, 2304, 128], P(None, 'mp', None, 'dp'), may hold values from 0.00025 to 330
- step_count: int32 [1], replicated, may hold values from 1 to 99999
- mlp_first: float32 [8, 4], replicated, may hold values from -2 to 2
- mlp_bias: float32 [4], replicated, may hold values from -3 to 3
- mlp_second: float32 [4, 2], replicated, may hold values from -3 to 3
- tensor_weight: float32 [10], replicated, may hold values from -2 to 2
Outputs:
- new_params: bfloat16 [64, 2, 2304, 128], P('mp')
- new_master: float32 [64, 2, 2304, 128], P('mp', None, 'dp')
- new_momenta: float32 [3, 64, 2, 2304, 128], P(None, 'mp', None, 'dp')
- new_second: float32 [3, 64, 2, 2304, 128], P(None, 'mp', None, 'dp')
- update: float32 [64, 2, 2304, 128], P('mp', None, 'dp')
All inputs are finite; a program needn't handle non-finite values.
Results may differ from a plain program's by a relative error of at most 0.019.
Values may be sent and summed in bfloat16 or wider, within the bound.
No kernel may reach another device: no remote copies, remote signals or barrier semaphores. Data moves between devices by JAX's collectives and lax.ppermute only.
A program may use at most 32 MiB of HBM per device.

v0:
```python
import functools

import jax
import jax.numpy as jnp
from jax import lax
from jax.sharding import Mesh
from jax.sharding import PartitionSpec as P

D = 4608
HQ = 4096
DP_MP = ("dp", "mp_0", "mp_1", "mp_2")
MP = ("mp_0", "mp_1", "mp_2")


RATES = (0.9, 0.99, 0.999)


def cut_along(x, dim, count):
    dims = x.shape
    blocks = x.reshape(*dims[:dim], count, dims[dim] // count, *dims[dim + 1 :])
    return jnp.moveaxis(blocks, dim, 0)


def sent_and_summed(x, axis, dim):
    count = lax.axis_size(axis)
    blocks = lax.all_to_all(cut_along(x, dim, count), axis, 0, 0, tiled=True)
    return jnp.sum(blocks.astype(jnp.float32), axis=0)


def over_axes(x, axes):
    return functools.reduce(lax.psum, axes, x)


def laid_out(blocks, dim):
    blocks = jnp.moveaxis(blocks, 0, dim)
    dims = blocks.shape
    return blocks.reshape(*dims[:dim], dims[dim] * dims[dim + 1], *dims[dim + 2 :])


def from_everyone(x, axis):
    copies = jnp.broadcast_to(x, (lax.axis_size(axis), *x.shape))
    return lax.all_to_all(copies, axis, split_axis=0, concat_axis=0, tiled=True)


def gather_directly(x, axis, dim):
    return laid_out(from_everyone(x, axis), dim)


def advance(gradient, momenta, second):
    moments = jnp.stack(
        [rate * momenta[i] + (1.0 - rate) * gradient for i, rate in enumerate(RATES)]
    )
    squares = jnp.stack(
        [rate * second[i] + (1.0 - rate) * gradient * gradient for i, rate in enumerate(RATES)]
    )
    return (moments, squares)


def features_of(master, gradient, moments, squares):
    listing = [master, gradient, moments[0], moments[1], moments[2]]
    for slot_id in range(3):
        listing.append(moments[slot_id] / jnp.sqrt(squares[slot_id]))
    return listing


def perceptron(normed, boost, mlp_first, mlp_bias, mlp_second):
    direction = jnp.zeros_like(normed[0])
    magnitude = jnp.zeros_like(normed[0])
    for unit_id in range(mlp_first.shape[1]):
        active = mlp_first[0, unit_id] * normed[0]
        for feat_id in range(1, len(normed)):
            active = active + mlp_first[feat_id, unit_id] * normed[feat_id]
        active = jax.nn.relu(active + mlp_bias[unit_id])
        direction = direction + mlp_second[unit_id, 0] * active
        magnitude = magnitude + mlp_second[unit_id, 1] * active
    return direction * jnp.exp(0.5 * jnp.tanh(magnitude)) * boost


def tensor_boost(norms, step_count, tensor_weight):
    count = tensor_weight.shape[0] - 2
    step_value = step_count[0].astype(jnp.float32)
    first_phase = jnp.log1p(step_value) / 11.5
    second_phase = step_value / 100000.0
    logits = jnp.sum(tensor_weight[:count, None] * jnp.log(norms), axis=0)
    logits = logits + tensor_weight[count] * first_phase + tensor_weight[count + 1] * second_phase
    return jnp.exp(jnp.tanh(logits))


def square_sums(listing):
    return jnp.stack([jnp.sum(feature * feature, axis=(0, 2, 3)) for feature in listing])


def local(
    grad_parts, master, momenta, second, step_count, mlp_first, mlp_bias, mlp_second, tensor_weight
):
    gradient = sent_and_summed(grad_parts, "dp", 3)[0]
    new_momenta, new_second = advance(gradient, momenta, second)
    early_local = square_sums([master, gradient])
    listing = features_of(master, gradient, new_momenta, new_second)
    late_local = square_sums(listing[2:])
    totals = over_axes(jnp.concatenate([early_local, late_local], axis=0), DP_MP)
    norms = jnp.sqrt(totals / float(D * HQ) + 1e-06)
    boost = tensor_boost(norms, step_count, tensor_weight)[None, :, None, None]
    normed = [listing[i] / norms[i][None, :, None, None] for i in range(len(listing))]
    update = perceptron(normed, boost, mlp_first, mlp_bias, mlp_second)
    new_master = master - 0.05 * update
    new_params = gather_directly(new_master.astype(jnp.bfloat16), "dp", 2)
    return (new_params, new_master, new_momenta, new_second, update)


def solution(mesh):
    torus = Mesh(mesh.devices.reshape(mesh.shape["dp"], 4, 8, 2), ("dp", "mp_0", "mp_1", "mp_2"))
    return jax.shard_map(
        local,
        mesh=torus,
        in_specs=(
            P("dp", MP, None, None, None),
            P(MP, None, "dp", None),
            P(None, MP, None, "dp", None),
            P(None, MP, None, "dp", None),
            P(),
            P(),
            P(),
            P(),
            P(),
        ),
        out_specs=(
            P(MP, None, None, None),
            P(MP, None, "dp", None),
            P(None, MP, None, "dp", None),
            P(None, MP, None, "dp", None),
            P(MP, None, "dp", None),
        ),
        check_vma=False,
    )
```

profile of v0, /device:TPU:64, one launch (start us, length us, event | category | flops | bytes accessed | tf_op | source)
XLA Modules:
  0.0 199.0 jit_solution(2062728544970626216)
XLA Ops:
  0.6 2.4 %copy.22 = bf16[12,1,1,2,192,128]{5,4,3,2,1,0:T(8,128)(2,1)} copy(bf16[12,1,1,2,192,128]{5,4,0,3,2,1:T(8,128)(2,1)} %bitcast.158) | data formatting | bytes 2359296 | tf_op jit(solution)/shard_map/transpose | solution.py:21
  3.0 0.0 copy-start.2
  3.0 0.0 copy-start.6
  3.0 0.0 copy-start.5
  3.0 0.0 copy-start.4
  3.0 0.0 copy-start.3
  3.0 14.9 %all-to-all-start = ((bf16[12,1,1,2,192,128]{5,4,3,2,1,0:T(8,128)(2,1)}), bf16[12,1,1,2,192,128]{5,4,3,2,1,0:T(8,128)(2,1)S(1)}, u32[]{:S(2)}, u32[]{:S(2)}) async-start(bf16[12,1,1,2,192,128]{5,4,3,2,1,0:T(8,128)(2,1)} %copy.22), calls=%async_computation | async-start | bytes 2359296 | tf_op jit(solution)/shard_map/all_to_all | solution.py:26
  18.0 0.0 copy-done.2
  18.0 0.0 copy-start
  18.0 0.0 copy-start.1
  18.0 0.1 multiply_reduce_fusion.7
  18.1 0.1 copy.23
  19.0 0.0 copy-done.6
  19.0 0.6 fusion.17
  20.9 0.0 copy-done.5
  20.9 0.7 fusion.16
  21.6 0.0 copy-done.4
  21.6 0.7 fusion.15
  22.3 0.0 copy-done.3
  22.3 0.7 fusion.14
  23.0 0.7 fusion.13
  23.7 39.4 %all-to-all-done = bf16[12,1,1,2,192,128]{5,4,3,2,1,0:T(8,128)(2,1)S(1)} async-done(((bf16[12,1,1,2,192,128]{5,4,3,2,1,0:T(8,128)(2,1)}), bf16[12,1,1,2,192,128]{5,4,3,2,1,0:T(8,128)(2,1)S(1)}, u32[]{:S(2)}, u32[]{:S(2)}) %all-to-all-start) | async-done | bytes 1179680 | tf_op jit(solution)/shard_map/all_to_all | solution.py:26
  63.1 0.2 convert_reduce_fusion
  63.2 0.1 multiply_reduce_fusion.6
  63.4 0.0 copy-done
  63.4 0.0 copy-done.1
  63.4 0.4 multiply_reduce_fusion
  63.7 0.1 copy.25
  63.8 0.1 copy.26
  63.9 0.1 copy.27
  64.0 0.1 copy.28
  64.1 0.1 copy.29
  64.2 0.1 copy.30
  64.3 0.1 copy.24
  64.4 0.1 concatenate.3
  64.5 19.9 %psum.28 = f32[8,2]{0,1:T(2,128)S(1)} all-reduce(f32[8,2]{0,1:T(2,128)S(1)} %concatenate.3), channel_id=1, replica_groups=mesh['dp'=12,'mp_0'=4,'mp_1'=8,'mp_2'=2] {'dp'}, use_global_device_ids=true, to_apply=%region_9.0 | all-reduce | flops 16 | bytes 128 | tf_op jit(solution)/shard_map/psum | solution.py:31
  84.4 10.5 %psum.29 = f32[8,2]{0,1:T(2,128)S(1)} all-reduce(f32[8,2]{0,1:T(2,128)S(1)} %psum.28), channel_id=1, replica_groups=mesh['dp'=12,'mp_0'=4,'mp_1'=8,'mp_2'=2] {'mp_0'}, use_global_device_ids=true, to_apply=%region_10.0 | all-reduce | flops 16 | bytes 128 | tf_op jit(solution)/shard_map/psum | solution.py:31
  94.9 17.6 %psum.30 = f32[8,2]{0,1:T(2,128)S(1)} all-reduce(f32[8,2]{0,1:T(2,128)S(1)} %psum.29), channel_id=1, replica_groups=mesh['dp'=12,'mp_0'=4,'mp_1'=8,'mp_2'=2] {'mp_1'}, use_global_device_ids=true, to_apply=%region_11.0 | all-reduce | flops 16 | bytes 128 | tf_op jit(solution)/shard_map/psum | solution.py:31
  112.5 2.5 %psum.31 = f32[8,2]{0,1:T(2,128)S(1)} all-reduce(f32[8,2]{0,1:T(2,128)S(1)} %psum.30), channel_id=1, replica_groups=mesh['dp'=12,'mp_0'=4,'mp_1'=8,'mp_2'=2] {'mp_2'}, use_global_device_ids=true, to_apply=%region_12.0 | all-reduce | flops 16 | bytes 128 | tf_op jit(solution)/shard_map/psum | solution.py:31
  115.0 0.1 fusion.12
  115.1 0.3 slice_reduce_fusion.7
  115.4 29.2 %convert_bitcast_fusion = (bf16[2,192,128]{2,1,0:T(8,128)(2,1)S(1)}, f32[1,2,192,128]{3,2,1,0:T(8,128)}, f32[1,2,192,128]{3,2,1,0:T(8,128)}) fusion(f32[1,2,192,128]{3,2,1,0:T(8,128)S(1)} %copy-done.2, f32[2]{0:T(128)S(1)} %tanh_exponential_fusion, f32[]{:T(128)} %bitcast.60, f32[]{:T(128)} %bitcast.59, f32[]{:T(128)} %bitcast.58, f32[]{:T(128)} %bitcast.57, ...), kind=kLoop, calls=%fused_computation.44 | loop fusion | flops 5750784 | bytes 2064632 | tf_op jit(solution)/shard_map/convert_element_type | solution.py:107
  144.6 1.3 broadcast_in_dim.2
  145.9 6.6 %all-to-all-start.1 = ((bf16[12,1,2,192,128]{4,3,2,1,0:T(8,128)(2,1)}), bf16[12,1,2,192,128]{4,3,2,1,0:T(8,128)(2,1)S(1)}, u32[]{:S(2)}, u32[]{:S(2)}) async-start(bf16[12,1,2,192,128]{4,3,2,1,0:T(8,128)(2,1)} %broadcast_in_dim.2), calls=%async_computation.1 | async-start | bytes 2359296 | tf_op jit(solution)/shard_map/all_to_all | solution.py:42
  152.5 0.2 fusion.9
  152.6 1.1 pad_maximum_fusion
  153.7 44.2 %all-to-all-done.1 = bf16[12,1,2,192,128]{4,3,2,1,0:T(8,128)(2,1)S(1)} async-done(((bf16[12,1,2,192,128]{4,3,2,1,0:T(8,128)(2,1)}), bf16[12,1,2,192,128]{4,3,2,1,0:T(8,128)(2,1)S(1)}, u32[]{:S(2)}, u32[]{:S(2)}) %all-to-all-start.1) | async-done | bytes 1179680 | tf_op jit(solution)/shard_map/all_to_all | solution.py:42
  197.9 1.1 copy.31
  (2 shorter events, 0.0 us)
Async XLA Ops:
  3.0 14.9 %copy-start.2 = (f32[1,2,192,128]{3,2,1,0:T(8,128)S(1)}, f32[1,2,192,128]{3,2,1,0:T(8,128)}, u32[]{:S(2)}) copy-start(f32[1,2,192,128]{3,2,1,0:T(8,128)} %param.10) | copy-start | bytes 589828
  3.0 16.0 %copy-start.6 = (f32[10]{0:T(128)S(1)}, f32[10]{0:T(128)}, u32[]{:S(2)}) copy-start(f32[10]{0:T(128)} %param.17) | copy-start | bytes 124
  3.0 17.9 %copy-start.5 = (f32[4]{0:T(128)S(1)}, f32[4]{0:T(128)}, u32[]{:S(2)}) copy-start(f32[4]{0:T(128)} %param.15) | copy-start | bytes 52
  3.0 18.6 %copy-start.4 = (f32[4,2]{0,1:T(2,128)S(1)}, f32[4,2]{0,1:T(2,128)}, u32[]{:S(2)}) copy-start(f32[4,2]{0,1:T(2,128)} %param.16) | copy-start | bytes 100
  3.0 19.2 %copy-start.3 = (f32[8,4]{0,1:T(4,128)S(1)}, f32[8,4]{0,1:T(4,128)}, u32[]{:S(2)}) copy-start(f32[8,4]{0,1:T(4,128)} %param.14) | copy-start | bytes 388
  3.0 60.0 %all-to-all-start = ((bf16[12,1,1,2,192,128]{5,4,3,2,1,0:T(8,128)(2,1)}), bf16[12,1,1,2,192,128]{5,4,3,2,1,0:T(8,128)(2,1)S(1)}, u32[]{:S(2)}, u32[]{:S(2)}) async-start(bf16[12,1,1,2,192,128]{5,4,3,2,1,0:T(8,128)(2,1)} %copy.22), calls=%async_computation | async-start | bytes 2359296 | tf_op jit(solution)/shard_map/all_to_all | solution.py:26
  18.0 45.4 %copy-start = (f32[3,1,2,192,128]{4,3,2,1,0:T(8,128)S(1)}, f32[3,1,2,192,128]{4,3,2,1,0:T(8,128)}, u32[]{:S(2)}) copy-start(f32[3,1,2,192,128]{4,3,2,1,0:T(8,128)} %param.12) | copy-start | bytes 1769476
  18.0 45.4 %copy-start.1 = (f32[3,1,2,192,128]{4,3,2,1,0:T(8,128)S(1)}, f32[3,1,2,192,128]{4,3,2,1,0:T(8,128)}, u32[]{:S(2)}) copy-start(f32[3,1,2,192,128]{4,3,2,1,0:T(8,128)} %param.11) | copy-start | bytes 1769476
  145.9 52.1 %all-to-all-start.1 = ((bf16[12,1,2,192,128]{4,3,2,1,0:T(8,128)(2,1)}), bf16[12,1,2,192,128]{4,3,2,1,0:T(8,128)(2,1)S(1)}, u32[]{:S(2)}, u32[]{:S(2)}) async-start(bf16[12,1,2,192,128]{4,3,2,1,0:T(8,128)(2,1)} %broadcast_in_dim.2), calls=%async_computation.1 | async-start | bytes 2359296 | tf_op jit(solution)/shard_map/all_to_all | solution.py:42
where the time goes:
time: 200 us; the launch traced here: 199 us
  waiting for transfers between devices  83.6 us (42%)
  blocking collectives  50.5 us (25%)
  other arithmetic  31.4 us (16%)
  starting transfers between devices  21.5 us (11%)
  local copies, waits for them, and re-layouts  9.25 us (5%)
  between operations  2.82 us (1%)
    psum x4, blocking collectives, over_axes(): return functools.reduce(lax.psum, axes, x)  50.5 us
    all_to_all x1, waiting for transfers between devices, from_everyone(): return lax.all_to_all(copies, axis, split_axis=0, concat_axis=0, tiled=True)  44.2 us
    all_to_all x1, waiting for transfers between devices, sent_and_summed(): blocks = lax.all_to_all(cut_along(x, dim, count), axis, 0, 0, tiled=True)  39.4 us
    convert_element_type x1, other arithmetic, local(): new_params = gather_directly(new_master.astype(jnp.bfloat16), 'dp', 2)  29.2 us
    all_to_all x1, starting transfers between devices, sent_and_summed(): blocks = lax.all_to_all(cut_along(x, dim, count), axis, 0, 0, tiled=True)  14.9 us
    all_to_all x1, starting transfers between devices, from_everyone(): return lax.all_to_all(copies, axis, split_axis=0, concat_axis=0, tiled=True)  6.6 us
  transfers between devices with their start and end apart: 2, of which 2 were waited for; matrix products, arithmetic and copies ran while one was open for 2% of the time, Pallas kernels for 0%

commit v1 on v0

v1 whole, which is shorter than its diff:
```python
import jax
import jax.numpy as jnp
from jax import lax
from jax.experimental import pallas as pl
from jax.experimental.pallas import tpu as pltpu
from jax.sharding import Mesh
from jax.sharding import PartitionSpec as P

D = 4608
HQ = 4096
DP = ("hi", "lo")
MP = ("mp_0", "mp_1", "mp_2")
RATES = (0.9, 0.99, 0.999)
FEATS = 8
HIDDEN = 4
NT = 2
LANES = 128
STEP = 32
LATE = 48

VMEM = pl.BlockSpec(memory_space=pltpu.VMEM)
SMEM = pl.BlockSpec(memory_space=pltpu.SMEM)


def ratio_of(moment, square):
    return moment * lax.rsqrt(square)


def reduced_gradient(parts):
    hi_count, lo_count = lax.axis_size("hi"), lax.axis_size("lo")
    count = hi_count * lo_count
    lo = lax.axis_index("lo")
    nt, rows, lanes = parts.shape
    blocks = parts.reshape(nt, hi_count, lo_count, rows // count, lanes)

    def of_class(shift):
        return lax.dynamic_index_in_dim(blocks, (lo + shift) % lo_count, 2, keepdims=False)

    from_below = lax.ppermute(of_class(1), DP, [(i, (i + 1) % count) for i in range(count)])
    from_above = lax.ppermute(of_class(lo_count - 1), DP, [(i, (i - 1) % count) for i in range(count)])
    partial = of_class(0).astype(jnp.float32) + from_below.astype(jnp.float32)
    partial = (partial + from_above.astype(jnp.float32)).astype(jnp.bfloat16)
    return lax.all_to_all(jnp.moveaxis(partial, 1, 0), "hi", 0, 0, tiled=True)


def moments_kernel(got, master, momenta, second, grad_out, momenta_out, second_out, sums_out, table):
    own = master.shape[0] // NT
    table[...] = jnp.zeros_like(table)
    for t in range(NT):

        def body(i, sums):
            rows = pl.ds(pl.multiple_of(t * own + i * STEP, STEP), STEP)
            grad = got[0, rows, :].astype(jnp.float32)
            for k in range(1, got.shape[0]):
                grad = grad + got[k, rows, :].astype(jnp.float32)
            grad_out[rows, :] = grad
            square = grad * grad
            listing = [master[rows, :], grad]
            ratios = []
            for k, rate in enumerate(RATES):
                moment = rate * momenta[k, rows, :] + (1.0 - rate) * grad
                spread = rate * second[k, rows, :] + (1.0 - rate) * square
                momenta_out[k, rows, :] = moment
                second_out[k, rows, :] = spread
                listing.append(moment)
                ratios.append(ratio_of(moment, spread))
            listing = listing + ratios
            return tuple(
                s + jnp.sum((x * x).reshape(STEP // 8, 8, LANES), axis=0)
                for s, x in zip(sums, listing)
            )

        zeros = tuple(jnp.zeros((8, LANES), jnp.float32) for _ in range(FEATS))
        sums = lax.fori_loop(0, own // STEP, body, zeros)
        for f in range(FEATS):
            k = t * FEATS + f
            table[k : k + 1, :] = jnp.sum(sums[f], axis=0, keepdims=True)
    sums_out[...] = lax.dot_general(
        jnp.ones(sums_out.shape, jnp.float32),
        table[...],
        (((1,), (1,)), ((), ())),
        precision=lax.Precision.HIGHEST,
        preferred_element_type=jnp.float32,
    )


def spread_kernel(got, out):
    out[...] = jnp.broadcast_to(jnp.sum(got[...], axis=0, keepdims=True), out.shape)


def update_kernel(
    totals, lane_weight, phase, first, bias, last, master, grad, momenta, second,
    update_out, master_out, params_out, late_out, scaled,
):
    own = master.shape[0] // NT
    early = params_out.shape[0]
    total = jnp.sum(totals[...], axis=0, keepdims=True)
    norms = jnp.sqrt(total / float(D * HQ) + 1e-06)
    inverse = 1.0 / norms
    logs = lane_weight[...] * jnp.log(norms)
    lane = lax.broadcasted_iota(jnp.int32, logs.shape, 1)
    for t in range(NT):
        mine = jnp.where(lane // FEATS == t, logs, 0.0)
        logit = jnp.sum(mine, axis=1, keepdims=True) + phase[0]
        boost = jnp.broadcast_to(jnp.exp(jnp.tanh(logit)), (8, LANES))
        for f in range(FEATS):
            k = t * FEATS + f
            scale = jnp.broadcast_to(inverse[:, k : k + 1], (8, LANES))
            for j in range(HIDDEN):
                scaled[f * HIDDEN + j] = first[f, j] * scale

        def rows_of(x):
            return jnp.broadcast_to(x[None], (STEP // 8, 8, LANES)).reshape(STEP, LANES)

        boost = rows_of(boost)

        def one(start):
            rows = pl.ds(start, STEP)
            old = master[rows, :]
            moments = [momenta[k, rows, :] for k in range(len(RATES))]
            listing = [old, grad[rows, :], *moments]
            listing += [ratio_of(moments[k], second[k, rows, :]) for k in range(len(RATES))]
            direction = jnp.zeros((STEP, LANES), jnp.float32)
            magnitude = jnp.zeros((STEP, LANES), jnp.float32)
            for j in range(HIDDEN):
                active = bias[j] + listing[0] * rows_of(scaled[j])
                for f in range(1, FEATS):
                    active = active + listing[f] * rows_of(scaled[f * HIDDEN + j])
                active = jnp.maximum(active, 0.0)
                direction = direction + last[j, 0] * active
                magnitude = magnitude + last[j, 1] * active
            step = direction * jnp.exp(0.5 * jnp.tanh(magnitude)) * boost
            new = old - 0.05 * step
            update_out[rows, :] = step
            master_out[rows, :] = new
            return new.astype(jnp.bfloat16)

        def body(i, carry):
            start = pl.multiple_of(t * own + i * STEP, STEP)
            params_out[pl.ds(start, STEP), :] = one(start)
            return carry

        last_early = min(early, (t + 1) * own)
        lax.fori_loop(0, (last_early - t * own) // STEP, body, 0)
        for start in range(last_early - (last_early - t * own) % STEP, (t + 1) * own, STEP):
            both = one(start)
            if start < early:
                params_out[start:early, :] = both[: early - start]
                both = both[early - start :]
            place = max(start, early) - early
            for copy in range(late_out.shape[0]):
                late_out[copy, place : place + both.shape[0], :] = both


def local(
    grad_parts, master, momenta, second, step_count, mlp_first, mlp_bias, mlp_second, tensor_weight
):
    dp_count = lax.axis_size("hi") * lax.axis_size("lo")
    mp_count = lax.axis_size("mp_0") * lax.axis_size("mp_1") * lax.axis_size("mp_2")
    _, nt, own, lanes = master.shape
    rows = nt * own
    early = rows - LATE
    f32 = jnp.float32
    state = jax.ShapeDtypeStruct((rows, lanes), f32)
    triple = jax.ShapeDtypeStruct((3, rows, lanes), f32)

    got = reduced_gradient(grad_parts[0, 0])
    old_master = master.reshape(rows, lanes)
    grad, new_momenta, new_second, sums = pl.pallas_call(
        moments_kernel,
        out_shape=(state, triple, triple, jax.ShapeDtypeStruct((mp_count, lanes), f32)),
        in_specs=[VMEM] * 4,
        out_specs=(VMEM,) * 4,
        scratch_shapes=[pltpu.VMEM((LANES, LANES), f32)],
        name="moments",
    )(
        got.reshape(-1, rows, lanes),
        old_master,
        momenta.reshape(3, rows, lanes),
        second.reshape(3, rows, lanes),
    )
    sums = lax.all_to_all(sums, MP, 0, 0, tiled=True)
    sums = pl.pallas_call(
        spread_kernel,
        out_shape=jax.ShapeDtypeStruct((dp_count, lanes), f32),
        in_specs=[VMEM],
        out_specs=VMEM,
        name="spread",
    )(sums)
    sums = lax.all_to_all(sums, DP, 0, 0, tiled=True)

    step_value = step_count[0].astype(f32)
    phase = tensor_weight[FEATS] * (jnp.log1p(step_value) / 11.5)
    phase = phase + tensor_weight[FEATS + 1] * (step_value / 100000.0)
    lane_weight = jnp.pad(jnp.tile(tensor_weight[:FEATS], nt), (0, lanes - nt * FEATS))[None]
    update, new_master, params, late = pl.pallas_call(
        update_kernel,
        out_shape=(
            state,
            state,
            jax.ShapeDtypeStruct((early, lanes), jnp.bfloat16),
            jax.ShapeDtypeStruct((dp_count, LATE, lanes), jnp.bfloat16),
        ),
        in_specs=[VMEM, VMEM, SMEM, SMEM, SMEM, SMEM, VMEM, VMEM, VMEM, VMEM],
        out_specs=(VMEM,) * 4,
        scratch_shapes=[pltpu.VMEM((FEATS * HIDDEN, 8, LANES), f32)],
        name="update",
    )(
        sums, lane_weight, phase[None], mlp_first, mlp_bias, mlp_second,
        old_master, grad, new_momenta, new_second,
    )
    late = lax.all_to_all(late, DP, 0, 0, tiled=True)
    params = lax.all_gather(params, DP, axis=0, tiled=False)
    second_part = jnp.concatenate([params[:, own:], late], axis=1)
    new_params = jnp.stack([params[:, :own], second_part]).reshape(1, nt, dp_count * own, lanes)
    shape = master.shape
    return (
        new_params,
        new_master.reshape(shape),
        new_momenta.reshape(3, *shape),
        new_second.reshape(3, *shape),
        update.reshape(shape),
    )


def solution(mesh):
    torus = Mesh(mesh.devices.reshape(mesh.shape["dp"] // 3, 3, 4, 8, 2), (*DP, *MP))
    return jax.shard_map(
        local,
        mesh=torus,
        in_specs=(
            P(DP, MP, None, None, None),
            P(MP, None, DP, None),
            P(None, MP, None, DP, None),
            P(None, MP, None, DP, None),
            P(),
            P(),
            P(),
            P(),
            P(),
        ),
        out_specs=(
            P(MP, None, None, None),
            P(MP, None, DP, None),
            P(None, MP, None, DP, None),
            P(None, MP, None, DP, None),
            P(MP, None, DP, None),
        ),
        check_vma=False,
    )
```

time: 200 us -> 133 us (0.67)
  the two profiles are of different devices: /device:TPU:64 before, /device:TPU:2 now
where the time goes in v1:
time: 133 us; the launch traced here: 132 us
  starting transfers between devices  41 us (31%)
  waiting for transfers between devices  40.8 us (31%)
  blocking collectives  30.6 us (23%)
  Pallas kernels  7.82 us (6%)
  local copies, waits for them, and re-layouts  7.28 us (5%)
  between operations  2.77 us (2%)
  other arithmetic  2.06 us (2%)
    all_gather x1, blocking collectives, local(): params = lax.all_gather(params, DP, axis=0, tiled=False)  30.6 us
    all_to_all x1, waiting for transfers between devices, reduced_gradient(): return lax.all_to_all(jnp.moveaxis(partial, 1, 0), 'hi', 0, 0, tiled=True)  18.3 us
    ppermute x1, starting transfers between devices, reduced_gradient(): lax.ppermute(of_class(lo_count - 1), DP, [(i, (i - 1) % count) for i in r...  12.2 us
    all_to_all x1, starting transfers between devices, local(): sums = lax.all_to_all(sums, MP, 0, 0, tiled=True)  10.7 us
    all_to_all x1, waiting for transfers between devices, local(): sums = lax.all_to_all(sums, MP, 0, 0, tiled=True)  7.93 us
    ppermute x1, waiting for transfers between devices, reduced_gradient(): lax.ppermute(of_class(1), DP, [(i, (i + 1) % count) for i in range(count)])  7.13 us
    all_to_all x1, starting transfers between devices, reduced_gradient(): return lax.all_to_all(jnp.moveaxis(partial, 1, 0), 'hi', 0, 0, tiled=True)  6.22 us
    all_to_all x1, waiting for transfers between devices, local(): sums = lax.all_to_all(sums, DP, 0, 0, tiled=True)  6.19 us
  transfers between devices with their start and end apart: 6, of which 5 were waited for; matrix products, arithmetic and copies ran while one was open for 2% of the time, Pallas kernels for 0%

profile of v1, /device:TPU:2, one launch (start us, length us, event | category | flops | bytes accessed | tf_op | source)
XLA Modules:
  0.0 132.3 jit_solution(11588265617088619656)
XLA Ops:
  0.7 1.3 %constant_dynamic-slice_fusion.2 = (bf16[2,4,1,192,128]{4,3,2,1,0:T(8,128)(2,1)S(1)}, bf16[2,4,1,192,128]{4,3,2,1,0:T(8,128)(2,1)S(1)}, bf16[2,4,1,192,128]{4,3,2,1,0:T(8,128)(2,1)S(1)}) fusion(bf16[2,4,3,192,128]{4,3,2,1,0:T(8,128)(2,1)} %bitcast.45, s32[]{:T(128)S(6)} %select_n.26, s32[]{:T(128)S(6)} %select_n.30, s32[]{:T(128)S(6)} %select_n.28), kind=kLoop, calls=%fused_computation.12 | loop fusion | bytes 2359308 | tf_op jit(solution)/shard_map/jit(dynamic_index_in_dim)/dynamic_slice | solution.py:37
  2.1 4.3 %collective-permute-start = (bf16[2,4,192,128]{3,2,0,1:T(8,128)(2,1)S(1)}, bf16[2,4,192,128]{3,2,0,1:T(8,128)(2,1)S(1)}, u32[]{:S(2)}, u32[]{:S(2)}) collective-permute-start(bf16[2,4,192,128]{3,2,0,1:T(8,128)(2,1)S(1)} %bitcast.52), channel_id=1, source_target_pairs={{0,64},{64,128},{128,192},{192,256},{256,320},{320,384},{384,448},... | collective-permute-start | bytes 1179656 | tf_op jit(solution)/shard_map/ppermute | solution.py:39
  6.4 12.2 %collective-permute-start.1 = (bf16[2,4,192,128]{3,2,0,1:T(8,128)(2,1)S(1)}, bf16[2,4,192,128]{3,2,0,1:T(8,128)(2,1)S(1)}, u32[]{:S(2)}, u32[]{:S(2)}) collective-permute-start(bf16[2,4,192,128]{3,2,0,1:T(8,128)(2,1)S(1)} %bitcast.53), channel_id=1, source_target_pairs={{0,704},{64,0},{128,64},{192,128},{256,192},{320,256},{384,320},{4... | collective-permute-start | bytes 1179656 | tf_op jit(solution)/shard_map/ppermute | solution.py:40
  18.6 7.1 %collective-permute-done = bf16[2,4,192,128]{3,2,0,1:T(8,128)(2,1)S(1)} collective-permute-done((bf16[2,4,192,128]{3,2,0,1:T(8,128)(2,1)S(1)}, bf16[2,4,192,128]{3,2,0,1:T(8,128)(2,1)S(1)}, u32[]{:S(2)}, u32[]{:S(2)}) %collective-permute-start) | collective-permute-done | bytes 393248 | tf_op jit(solution)/shard_map/ppermute | solution.py:39
  25.8 1.2 collective-permute-done.1
  27.0 0.0 copy-start.3
  27.0 0.9 fusion.2
  27.9 0.0 copy-start.4
  27.9 0.0 copy-start.2
  27.9 6.2 %all-to-all-start = ((bf16[4,2,192,128]{3,2,1,0:T(8,128)(2,1)}), bf16[4,2,192,128]{3,2,1,0:T(8,128)(2,1)S(1)}, u32[]{:S(2)}, u32[]{:S(2)}) async-start(bf16[4,2,192,128]{3,2,1,0:T(8,128)(2,1)} %fusion.2), calls=%async_computation | async-start | bytes 786432 | tf_op jit(solution)/shard_map/all_to_all | solution.py:43
  34.1 0.0 copy-done.3
  34.1 0.1 tile.10
  34.2 18.3 %all-to-all-done = bf16[4,2,192,128]{3,2,1,0:T(8,128)(2,1)S(1)} async-done(((bf16[4,2,192,128]{3,2,1,0:T(8,128)(2,1)}), bf16[4,2,192,128]{3,2,1,0:T(8,128)(2,1)S(1)}, u32[]{:S(2)}, u32[]{:S(2)}) %all-to-all-start) | async-done | bytes 393248 | tf_op jit(solution)/shard_map/all_to_all | solution.py:43
  52.5 0.0 copy-start
  52.5 0.7 copy-done
  53.3 3.0 %moments.1 = (f32[384,128]{1,0:T(8,128)}, f32[3,384,128]{2,1,0:T(8,128)}, f32[3,384,128]{2,1,0:T(8,128)}, f32[64,128]{1,0:T(8,128)}) custom-call(bf16[4,384,128]{2,1,0:T(8,128)(2,1)} %bitcast.44, f32[384,128]{1,0:T(8,128)} %bitcast.46, f32[3,384,128]{2,1,0:T(8,128)} %bitcast.48, f32[3,384,128]{2,1,0:T(8,128)} %bitcast.49), custom_call_target="tpu_custom_call" | custom-call | tf_op jit(solution)/shard_map/moments/pallas_call | solution.py:169
  56.2 10.7 %all-to-all-start.1 = ((f32[64,1,128]{2,1,0:T(1,128)}), f32[64,1,128]{2,1,0:T(1,128)S(1)}, u32[]{:S(2)}, u32[]{:S(2)}) async-start(f32[64,1,128]{2,1,0:T(1,128)} %bitcast.57), calls=%async_computation.1 | async-start | bytes 65536 | tf_op jit(solution)/shard_map/all_to_all | solution.py:182
  66.9 0.6 fusion.3
  67.5 7.9 %all-to-all-done.1 = f32[64,1,128]{2,1,0:T(1,128)S(1)} async-done(((f32[64,1,128]{2,1,0:T(1,128)}), f32[64,1,128]{2,1,0:T(1,128)S(1)}, u32[]{:S(2)}, u32[]{:S(2)}) %all-to-all-start.1) | async-done | bytes 32800 | tf_op jit(solution)/shard_map/all_to_all | solution.py:182
  75.4 0.0 copy-start.1
  75.4 0.6 copy-done.1
  76.1 1.4 %spread.1 = f32[12,128]{1,0:T(8,128)} custom-call(f32[64,128]{1,0:T(8,128)} %bitcast.54), custom_call_target="tpu_custom_call" | custom-call | tf_op jit(solution)/shard_map/spread/pallas_call | solution.py:183
  77.4 1.3 copy.25
  78.7 4.1 %all-to-all-start.2 = ((f32[12,1,128]{2,1,0:T(1,128)}), f32[12,1,128]{2,1,0:T(1,128)S(1)}, u32[]{:S(2)}, u32[]{:S(2)}) async-start(f32[12,1,128]{2,1,0:T(1,128)} %copy.25), calls=%async_computation.2 | async-start | bytes 12288 | tf_op jit(solution)/shard_map/all_to_all | solution.py:190
  82.9 0.5 pad_bitcast_fusion.lane_weight
  84.1 0.0 copy-done.4
  84.1 0.7 copy.27.last
  84.8 0.0 copy-done.2
  84.8 0.7 copy.26.first
  86.7 6.2 %all-to-all-done.2 = f32[12,1,128]{2,1,0:T(1,128)S(1)} async-done(((f32[12,1,128]{2,1,0:T(1,128)}), f32[12,1,128]{2,1,0:T(1,128)S(1)}, u32[]{:S(2)}, u32[]{:S(2)}) %all-to-all-start.2) | async-done | bytes 6176 | tf_op jit(solution)/shard_map/all_to_all | solution.py:190
  92.9 0.6 copy.40
  93.5 3.5 %update.1 = (f32[384,128]{1,0:T(8,128)}, f32[384,128]{1,0:T(8,128)}, bf16[336,128]{1,0:T(8,128)(2,1)}, bf16[12,48,128]{2,1,0:T(8,128)(2,1)}) custom-call(f32[12,128]{1,0:T(8,128)} %bitcast.55, f32[1,128]{1,0:T(1,128)} %pad_bitcast_fusion.lane_weight, f32[1]{0:T(128)S(6)} %add.48.phase, f32[8,4]{1,0:T(8,128)} %copy.26.first, f32[4]{0:T(128)} %bias.1, ...), custom_call_target="tpu_custom_call" | custom-call | tf_op jit(solution)/shard_map/update/pallas_call | solution.py:196
  97.0 3.5 %all-to-all-start.3 = ((bf16[12,48,128]{2,1,0:T(8,128)(2,1)}), bf16[12,48,128]{2,1,0:T(8,128)(2,1)S(1)}, u32[]{:S(2)}, u32[]{:S(2)}) async-start(bf16[12,48,128]{2,1,0:T(8,128)(2,1)} %get-tuple-element.18), calls=%async_computation.3 | async-start | bytes 294912 | tf_op jit(solution)/shard_map/all_to_all | solution.py:212
  100.5 30.6 %all-gather = bf16[4032,128]{1,0:T(8,128)(2,1)S(1)} all-gather(bf16[336,128]{1,0:T(8,128)(2,1)} %get-tuple-element.17), channel_id=2, replica_groups=mesh['hi'=4,'lo'=3,'mp_0'=4,'mp_1'=8,'mp_2'=2] {'hi','lo'}, dimensions={0}, use_global_device_ids=true | all-gather | bytes 1118208 | tf_op jit(solution)/shard_map/all_gather | solution.py:213
  131.2 0.0 all-to-all-done.3
  131.2 1.1 pad_maximum_fusion
  (6 shorter events, 0.2 us)
Async XLA Ops:
  2.1 23.7 %collective-permute-start = (bf16[2,4,192,128]{3,2,0,1:T(8,128)(2,1)S(1)}, bf16[2,4,192,128]{3,2,0,1:T(8,128)(2,1)S(1)}, u32[]{:S(2)}, u32[]{:S(2)}) collective-permute-start(bf16[2,4,192,128]{3,2,0,1:T(8,128)(2,1)S(1)} %bitcast.52), channel_id=1, source_target_pairs={{0,64},{64,128},{128,192},{192,256},{256,320},{320,384},{384,448},... | collective-permute-start | bytes 1179656 | tf_op jit(solution)/shard_map/ppermute | solution.py:39
  6.4 20.6 %collective-permute-start.1 = (bf16[2,4,192,128]{3,2,0,1:T(8,128)(2,1)S(1)}, bf16[2,4,192,128]{3,2,0,1:T(8,128)(2,1)S(1)}, u32[]{:S(2)}, u32[]{:S(2)}) collective-permute-start(bf16[2,4,192,128]{3,2,0,1:T(8,128)(2,1)S(1)} %bitcast.53), channel_id=1, source_target_pairs={{0,704},{64,0},{128,64},{192,128},{256,192},{320,256},{384,320},{4... | collective-permute-start | bytes 1179656 | tf_op jit(solution)/shard_map/ppermute | solution.py:40
  27.0 7.1 %copy-start.3 = (f32[10]{0:T(128)S(1)}, f32[10]{0:T(128)}, u32[]{:S(2)}) copy-start(f32[10]{0:T(128)} %param.17) | copy-start | bytes 124
  27.9 56.2 %copy-start.4 = (f32[4,2]{0,1:T(2,128)S(1)}, f32[4,2]{0,1:T(2,128)}, u32[]{:S(2)}) copy-start(f32[4,2]{0,1:T(2,128)} %param.16) | copy-start | bytes 100
  27.9 56.9 %copy-start.2 = (f32[8,4]{0,1:T(4,128)S(1)}, f32[8,4]{0,1:T(4,128)}, u32[]{:S(2)}) copy-start(f32[8,4]{0,1:T(4,128)} %param.14) | copy-start | bytes 388
  27.9 24.6 %all-to-all-start = ((bf16[4,2,192,128]{3,2,1,0:T(8,128)(2,1)}), bf16[4,2,192,128]{3,2,1,0:T(8,128)(2,1)S(1)}, u32[]{:S(2)}, u32[]{:S(2)}) async-start(bf16[4,2,192,128]{3,2,1,0:T(8,128)(2,1)} %fusion.2), calls=%async_computation | async-start | bytes 786432 | tf_op jit(solution)/shard_map/all_to_all | solution.py:43
  52.5 0.7 copy-start
  56.2 19.2 %all-to-all-start.1 = ((f32[64,1,128]{2,1,0:T(1,128)}), f32[64,1,128]{2,1,0:T(1,128)S(1)}, u32[]{:S(2)}, u32[]{:S(2)}) async-start(f32[64,1,128]{2,1,0:T(1,128)} %bitcast.57), calls=%async_computation.1 | async-start | bytes 65536 | tf_op jit(solution)/shard_map/all_to_all | solution.py:182
  75.4 0.6 copy-start.1
  78.7 14.2 %all-to-all-start.2 = ((f32[12,1,128]{2,1,0:T(1,128)}), f32[12,1,128]{2,1,0:T(1,128)S(1)}, u32[]{:S(2)}, u32[]{:S(2)}) async-start(f32[12,1,128]{2,1,0:T(1,128)} %copy.25), calls=%async_computation.2 | async-start | bytes 12288 | tf_op jit(solution)/shard_map/all_to_all | solution.py:190
  97.0 34.2 %all-to-all-start.3 = ((bf16[12,48,128]{2,1,0:T(8,128)(2,1)}), bf16[12,48,128]{2,1,0:T(8,128)(2,1)S(1)}, u32[]{:S(2)}, u32[]{:S(2)}) async-start(bf16[12,48,128]{2,1,0:T(8,128)(2,1)} %get-tuple-element.18), calls=%async_computation.3 | async-start | bytes 294912 | tf_op jit(solution)/shard_map/all_to_all | solution.py:212

commit v2 on v1

v2 whole, which is shorter than its diff:
```python
import jax
import jax.numpy as jnp
from jax import lax
from jax.experimental import pallas as pl
from jax.experimental.pallas import tpu as pltpu
from jax.sharding import Mesh
from jax.sharding import PartitionSpec as P

D = 4608
HQ = 4096
DP = ("hi", "lo")
MP = ("mp_0", "mp_1", "mp_2")
RATES = (0.9, 0.99, 0.999)
FEATS = 8
HIDDEN = 4
NT = 2
LANES = 128
STEP = 32
TAIL = 16
GRADES = 8

VMEM = pl.BlockSpec(memory_space=pltpu.VMEM)
SMEM = pl.BlockSpec(memory_space=pltpu.SMEM)
PARAMS = pltpu.CompilerParams(vmem_limit_bytes=6 << 20)


def reduced_gradient(parts):
    hi_count, lo_count = lax.axis_size("hi"), lax.axis_size("lo")
    count = hi_count * lo_count
    lo = lax.axis_index("lo")
    nt, rows, lanes = parts.shape
    blocks = parts.reshape(nt, hi_count, lo_count, rows // count, lanes)

    def of_class(shift):
        return lax.dynamic_index_in_dim(blocks, (lo + shift) % lo_count, 2, keepdims=False)

    from_below = lax.ppermute(of_class(1), DP, [(i, (i + 1) % count) for i in range(count)])
    from_above = lax.ppermute(of_class(lo_count - 1), DP, [(i, (i - 1) % count) for i in range(count)])
    partial = of_class(0).astype(jnp.float32) + from_below.astype(jnp.float32)
    partial = (partial + from_above.astype(jnp.float32)).astype(jnp.bfloat16)
    return lax.all_to_all(jnp.moveaxis(partial, 1, 0), "hi", 0, 0, tiled=True)


def moments_kernel(got, master, momenta, second, features_out, sums_out, table):
    own = master.shape[0] // NT
    table[...] = jnp.zeros_like(table)
    for t in range(NT):

        def body(i, sums):
            rows = pl.ds(pl.multiple_of(t * own + i * STEP, STEP), STEP)
            grad = got[0, rows, :].astype(jnp.float32)
            for k in range(1, got.shape[0]):
                grad = grad + got[k, rows, :].astype(jnp.float32)
            square = grad * grad
            moments, ratios = [], []
            for k, rate in enumerate(RATES):
                moment = rate * momenta[k, rows, :] + (1.0 - rate) * grad
                spread = rate * second[k, rows, :] + (1.0 - rate) * square
                moments.append(moment)
                ratios.append(moment * lax.rsqrt(spread))
            listing = [grad, *moments, *ratios]
            for k, x in enumerate(listing):
                features_out[k, rows, :] = x
            return tuple(
                s + jnp.sum((x * x).reshape(STEP // 8, 8, LANES), axis=0)
                for s, x in zip(sums, [master[rows, :], *listing])
            )

        zeros = tuple(jnp.zeros((8, LANES), jnp.float32) for _ in range(FEATS))
        sums = lax.fori_loop(0, own // STEP, body, zeros)
        for f in range(FEATS):
            k = t * FEATS + f
            table[k : k + 1, :] = jnp.sum(sums[f], axis=0, keepdims=True)
    sums_out[...] = lax.dot_general(
        jnp.ones(sums_out.shape, jnp.float32),
        table[...],
        (((1,), (1,)), ((), ())),
        precision=lax.Precision.HIGHEST,
        preferred_element_type=jnp.float32,
    )


def update_kernel(
    totals, lane_weight, phase, first, bias, last, master, features,
    update_out, master_out, params_out, scaled,
):
    rows = master.shape[0]
    own = rows // NT
    total = jnp.sum(totals[...], axis=0, keepdims=True)
    norms = jnp.sqrt(total / float(D * HQ) + 1e-06)
    inverse = 1.0 / norms
    logs = lane_weight[...] * jnp.log(norms)
    lane = lax.broadcasted_iota(jnp.int32, logs.shape, 1)

    def rows_of(x):
        return jnp.broadcast_to(x[None], (STEP // 8, 8, LANES)).reshape(STEP, LANES)

    largest = jnp.zeros((8, LANES), jnp.float32)
    for t in range(NT):
        mine = jnp.where(lane // FEATS == t, logs, 0.0)
        logit = jnp.sum(mine, axis=1, keepdims=True) + phase[0]
        boost = rows_of(jnp.broadcast_to(jnp.exp(jnp.tanh(logit)), (8, LANES)))
        for f in range(FEATS):
            k = t * FEATS + f
            scale = jnp.broadcast_to(inverse[:, k : k + 1], (8, LANES))
            for j in range(HIDDEN):
                scaled[f * HIDDEN + j] = first[f, j] * scale

        def body(i, largest):
            at = pl.ds(pl.multiple_of(t * own + i * STEP, STEP), STEP)
            old = master[at, :]
            listing = [old] + [features[k, at, :] for k in range(FEATS - 1)]
            direction = jnp.zeros((STEP, LANES), jnp.float32)
            magnitude = jnp.zeros((STEP, LANES), jnp.float32)
            for j in range(HIDDEN):
                active = bias[j] + listing[0] * rows_of(scaled[j])
                for f in range(1, FEATS):
                    active = active + listing[f] * rows_of(scaled[f * HIDDEN + j])
                active = jnp.maximum(active, 0.0)
                direction = direction + last[j, 0] * active
                magnitude = magnitude + last[j, 1] * active
            step = direction * jnp.exp(0.5 * jnp.tanh(magnitude)) * boost
            new = old - 0.05 * step
            update_out[at, :] = step
            master_out[at, :] = new
            return jnp.maximum(largest, jnp.max(jnp.abs(new).reshape(STEP // 8, 8, LANES), axis=0))

        largest = lax.fori_loop(0, own // STEP, body, largest)

    most = jnp.max(jnp.max(largest, axis=0, keepdims=True), axis=1, keepdims=True) * 0.125
    power = jnp.full((1, 1), 0.125, jnp.float32)
    grades = jnp.ones((1, LANES), jnp.float32)
    for k in range(GRADES):
        small = most < 8.0
        most = jnp.where(small, most * 4096.0, most)
        power = jnp.where(small, power * 4096.0, power)
        grades = jnp.where(jnp.logical_and(small, lane == k), 1.0 / 4096.0, grades)
    power = jnp.broadcast_to(power, (STEP, LANES))

    def write(i, carry):
        at = pl.ds(pl.multiple_of(i * STEP, STEP), STEP)
        rounded = master_out[at, :].astype(jnp.bfloat16).astype(jnp.float32)
        params_out[at, :] = (rounded * power).astype(params_out.dtype)
        return carry

    lax.fori_loop(0, rows // STEP, write, 0)
    params_out[rows:, :] = jnp.broadcast_to(grades, (TAIL, LANES)).astype(params_out.dtype)


def local(
    grad_parts, master, momenta, second, step_count, mlp_first, mlp_bias, mlp_second, tensor_weight
):
    dp_count = lax.axis_size("hi") * lax.axis_size("lo")
    mp_count = lax.axis_size("mp_0") * lax.axis_size("mp_1") * lax.axis_size("mp_2")
    _, nt, own, lanes = master.shape
    rows = nt * own
    f32, bf16 = jnp.float32, jnp.bfloat16
    state = jax.ShapeDtypeStruct((rows, lanes), f32)

    got = reduced_gradient(grad_parts[0, 0])
    old_master = master.reshape(rows, lanes)
    old_second = second.reshape(3, rows, lanes)
    features, sums = pl.pallas_call(
        moments_kernel,
        out_shape=(
            jax.ShapeDtypeStruct((FEATS - 1, rows, lanes), f32),
            jax.ShapeDtypeStruct((mp_count, lanes), f32),
        ),
        in_specs=[VMEM] * 4,
        out_specs=(VMEM,) * 2,
        scratch_shapes=[pltpu.VMEM((LANES, LANES), f32)],
        compiler_params=PARAMS,
        name="moments",
    )(got.reshape(-1, rows, lanes), old_master, momenta.reshape(3, rows, lanes), old_second)
    sums = lax.all_to_all(sums, MP, 0, 0, tiled=True)
    sums = jnp.broadcast_to(jnp.sum(sums, axis=0), (dp_count, lanes))
    sums = lax.all_to_all(sums, DP, 0, 0, tiled=True)

    new_momenta = features[1:4]
    square = features[0] * features[0]
    new_second = jnp.stack(
        [rate * old_second[k] + (1.0 - rate) * square for k, rate in enumerate(RATES)]
    )

    step_value = step_count[0].astype(f32)
    phase = tensor_weight[FEATS] * (jnp.log1p(step_value) / 11.5)
    phase = phase + tensor_weight[FEATS + 1] * (step_value / 100000.0)
    lane_weight = jnp.pad(jnp.tile(tensor_weight[:FEATS], nt), (0, lanes - nt * FEATS))[None]
    update, new_master, params = pl.pallas_call(
        update_kernel,
        out_shape=(state, state, jax.ShapeDtypeStruct((rows + TAIL, lanes), bf16)),
        in_specs=[VMEM, VMEM, SMEM, SMEM, SMEM, SMEM, VMEM, VMEM],
        out_specs=(VMEM,) * 3,
        scratch_shapes=[pltpu.VMEM((FEATS * HIDDEN, 8, LANES), f32)],
        compiler_params=PARAMS,
        name="update",
    )(sums, lane_weight, phase[None], mlp_first, mlp_bias, mlp_second, old_master, features)
    params = lax.all_gather(params.astype(jnp.float16), DP, axis=0, tiled=False)
    scale = 8.0 * jnp.prod(params[:, rows, :GRADES].astype(f32), axis=1)
    params = params[:, :rows].astype(f32) * scale[:, None, None]
    params = params.astype(bf16).reshape(dp_count, nt, own, lanes)
    new_params = jnp.moveaxis(params, 0, 1).reshape(1, nt, dp_count * own, lanes)
    shape = master.shape
    return (
        new_params,
        new_master.reshape(shape),
        new_momenta.reshape(3, *shape),
        new_second.reshape(3, *shape),
        update.reshape(shape),
    )


def solution(mesh):
    torus = Mesh(mesh.devices.reshape(mesh.shape["dp"] // 3, 3, 4, 8, 2), (*DP, *MP))
    return jax.shard_map(
        local,
        mesh=torus,
        in_specs=(
            P(DP, MP, None, None, None),
            P(MP, None, DP, None),
            P(None, MP, None, DP, None),
            P(None, MP, None, DP, None),
            P(),
            P(),
            P(),
            P(),
            P(),
        ),
        out_specs=(
            P(MP, None, None, None),
            P(MP, None, DP, None),
            P(None, MP, None, DP, None),
            P(None, MP, None, DP, None),
            P(MP, None, DP, None),
        ),
        check_vma=False,
    )
```

time: 133 us -> 122 us (0.917)
  Pallas kernels: 7.82 us -> 3.88 us
  starting transfers between devices: 41 us -> 37.6 us
  local copies, waits for them, and re-layouts: 7.28 us -> 4.81 us
  other arithmetic: 2.06 us -> 4.25 us
  blocking collectives: 30.6 us -> 28.7 us
  waiting for transfers between devices: 40.8 us -> 39 us
    all_to_all x1, waiting for transfers between devices: 18.3 us -> 14.8 us  [reduced_gradient(): return lax.all_to_all(jnp.moveaxis(partial, 1, 0), 'hi', 0, 0, tiled=True)]
    all_to_all x1 -> x0, starting transfers between devices: 3.52 us -> none  [local(): late = lax.all_to_all(late, DP, 0, 0, tiled=True)]
    unnamed x13 -> x17, local copies, waits for them, and re-layouts: 3.3 us -> 0.21 us
    pallas_call x2 -> x1, Pallas kernels: 4.33 us -> 1.31 us  [local(): pl.pallas_call(moments_kernel, out_shape=(jax.ShapeDtypeStruct((FEATS - 1...]
    all_to_all x1, waiting for transfers between devices: 6.19 us -> 8.3 us  [local(): sums = lax.all_to_all(sums, DP, 0, 0, tiled=True)]
    all_gather x1, blocking collectives: 30.6 us -> 28.7 us  [local(): params = lax.all_gather(params.astype(jnp.float16), DP, axis=0, tiled=False)]
  transfers between devices with their start and end apart: 6 -> 5, of which waited for: 5 -> 5; matrix products, arithmetic and copies ran while one was open for 2% -> 4% of each run, Pallas kernels for 0% -> 0%
where the time goes in v2:
time: 122 us; the launch traced here: 121 us
  waiting for transfers between devices  39 us (32%)
  starting transfers between devices  37.6 us (31%)
  blocking collectives  28.7 us (24%)
  local copies, waits for them, and re-layouts  4.81 us (4%)
  other arithmetic  4.25 us (3%)
  Pallas kernels  3.88 us (3%)
  between operations  2.84 us (2%)
    all_gather x1, blocking collectives, local(): params = lax.all_gather(params.astype(jnp.float16), DP, axis=0, tiled=False)  28.7 us
    all_to_all x1, waiting for transfers between devices, reduced_gradient(): return lax.all_to_all(jnp.moveaxis(partial, 1, 0), 'hi', 0, 0, tiled=True)  14.8 us
    ppermute x1, starting transfers between devices, reduced_gradient(): lax.ppermute(of_class(lo_count - 1), DP, [(i, (i - 1) % count) for i in r...  12.4 us
    all_to_all x1, starting transfers between devices, local(): sums = lax.all_to_all(sums, MP, 0, 0, tiled=True)  10.7 us
    all_to_all x1, waiting for transfers between devices, local(): sums = lax.all_to_all(sums, DP, 0, 0, tiled=True)  8.3 us
    all_to_all x1, waiting for transfers between devices, local(): sums = lax.all_to_all(sums, MP, 0, 0, tiled=True)  7.54 us
    ppermute x1, waiting for transfers between devices, reduced_gradient(): lax.ppermute(of_class(1), DP, [(i, (i + 1) % count) for i in range(count)])  6.95 us
    all_to_all x1, starting transfers between devices, reduced_gradient(): return lax.all_to_all(jnp.moveaxis(partial, 1, 0), 'hi', 0, 0, tiled=True)  6.22 us
  transfers between devices with their start and end apart: 5, of which 5 were waited for; matrix products, arithmetic and copies ran while one was open for 4% of the time, Pallas kernels for 0%

profile of v2, /device:TPU:2, one launch (start us, length us, event | category | flops | bytes accessed | tf_op | source)
XLA Modules:
  0.0 121.1 jit_solution(7199479333097542523)
XLA Ops:
  0.7 1.3 %constant_dynamic-slice_fusion.2 = (bf16[2,4,1,192,128]{4,3,2,1,0:T(8,128)(2,1)S(1)}, bf16[2,4,1,192,128]{4,3,2,1,0:T(8,128)(2,1)S(1)}, bf16[2,4,1,192,128]{4,3,2,1,0:T(8,128)(2,1)S(1)}) fusion(bf16[2,4,3,192,128]{4,3,2,1,0:T(8,128)(2,1)} %bitcast.55, s32[]{:T(128)S(6)} %select_n.26, s32[]{:T(128)S(6)} %select_n.30, s32[]{:T(128)S(6)} %select_n.28), kind=kLoop, calls=%fused_computation.21 | loop fusion | bytes 2359308 | tf_op jit(solution)/shard_map/jit(dynamic_index_in_dim)/dynamic_slice | solution.py:35
  2.1 4.3 %collective-permute-start = (bf16[2,4,192,128]{3,2,0,1:T(8,128)(2,1)S(1)}, bf16[2,4,192,128]{3,2,0,1:T(8,128)(2,1)S(1)}, u32[]{:S(2)}, u32[]{:S(2)}) collective-permute-start(bf16[2,4,192,128]{3,2,0,1:T(8,128)(2,1)S(1)} %bitcast.61), channel_id=1, source_target_pairs={{0,64},{64,128},{128,192},{192,256},{256,320},{320,384},{384,448},... | collective-permute-start | bytes 1179656 | tf_op jit(solution)/shard_map/ppermute | solution.py:37
  6.4 0.0 copy-start.5
  6.4 0.0 copy-start.6
  6.4 0.0 copy-start.4
  6.4 0.0 copy-start
  6.4 12.4 %collective-permute-start.1 = (bf16[2,4,192,128]{3,2,0,1:T(8,128)(2,1)S(1)}, bf16[2,4,192,128]{3,2,0,1:T(8,128)(2,1)S(1)}, u32[]{:S(2)}, u32[]{:S(2)}) collective-permute-start(bf16[2,4,192,128]{3,2,0,1:T(8,128)(2,1)S(1)} %bitcast.62), channel_id=1, source_target_pairs={{0,704},{64,0},{128,64},{192,128},{256,192},{320,256},{384,320},{4... | collective-permute-start | bytes 1179656 | tf_op jit(solution)/shard_map/ppermute | solution.py:38
  18.8 7.0 %collective-permute-done = bf16[2,4,192,128]{3,2,0,1:T(8,128)(2,1)S(1)} collective-permute-done((bf16[2,4,192,128]{3,2,0,1:T(8,128)(2,1)S(1)}, bf16[2,4,192,128]{3,2,0,1:T(8,128)(2,1)S(1)}, u32[]{:S(2)}, u32[]{:S(2)}) %collective-permute-start) | collective-permute-done | bytes 393248 | tf_op jit(solution)/shard_map/ppermute | solution.py:37
  25.8 1.4 %collective-permute-done.1 = bf16[2,4,192,128]{3,2,0,1:T(8,128)(2,1)S(1)} collective-permute-done((bf16[2,4,192,128]{3,2,0,1:T(8,128)(2,1)S(1)}, bf16[2,4,192,128]{3,2,0,1:T(8,128)(2,1)S(1)}, u32[]{:S(2)}, u32[]{:S(2)}) %collective-permute-start.1) | collective-permute-done | bytes 393248 | tf_op jit(solution)/shard_map/ppermute | solution.py:38
  27.1 0.9 fusion.2
  28.0 0.0 copy-start.1
  28.1 0.0 copy-start.2
  28.1 6.2 %all-to-all-start = ((bf16[4,2,192,128]{3,2,1,0:T(8,128)(2,1)}), bf16[4,2,192,128]{3,2,1,0:T(8,128)(2,1)S(1)}, u32[]{:S(2)}, u32[]{:S(2)}) async-start(bf16[4,2,192,128]{3,2,1,0:T(8,128)(2,1)} %fusion.2), calls=%async_computation | async-start | bytes 786432 | tf_op jit(solution)/shard_map/all_to_all | solution.py:41
  35.0 0.0 copy-done.5
  35.0 0.1 tile.10
  35.1 0.0 copy-done.6
  35.1 0.1 copy.26.last
  35.2 0.0 copy-done.4
  35.2 0.1 copy.25.first
  35.3 0.6 fusion.4
  37.2 0.0 copy-done
  37.2 0.7 slice_multiply_fusion.3
  37.9 14.8 %all-to-all-done = bf16[4,2,192,128]{3,2,1,0:T(8,128)(2,1)S(1)} async-done(((bf16[4,2,192,128]{3,2,1,0:T(8,128)(2,1)}), bf16[4,2,192,128]{3,2,1,0:T(8,128)(2,1)S(1)}, u32[]{:S(2)}, u32[]{:S(2)}) %all-to-all-start) | async-done | bytes 393248 | tf_op jit(solution)/shard_map/all_to_all | solution.py:41
  52.7 0.0 copy-done.1
  52.7 0.0 copy-done.2
  52.7 1.3 %moments.1 = (f32[7,384,128]{2,1,0:T(8,128)S(1)}, f32[64,128]{1,0:T(8,128)}) custom-call(bf16[4,384,128]{2,1,0:T(8,128)(2,1)S(1)} %bitcast.47, f32[384,128]{1,0:T(8,128)S(1)} %bitcast.48, f32[3,384,128]{2,1,0:T(8,128)S(1)} %bitcast.50, f32[3,384,128]{2,1,0:T(8,128)S(1)} %bitcast.46), custom_call_target="tpu_custom_call" | custom-call | tf_op jit(solution)/shard_map/moments/pallas_call | solution.py:163
  54.0 10.7 %all-to-all-start.1 = ((f32[64,1,128]{2,1,0:T(1,128)}), f32[64,1,128]{2,1,0:T(1,128)S(1)}, u32[]{:S(2)}, u32[]{:S(2)}) async-start(f32[64,1,128]{2,1,0:T(1,128)} %bitcast.10), calls=%async_computation.1 | async-start | bytes 65536 | tf_op jit(solution)/shard_map/all_to_all | solution.py:175
  64.7 1.0 bitcast_add_fusion.2
  65.7 0.0 copy-start.3
  65.7 7.5 %all-to-all-done.1 = f32[64,1,128]{2,1,0:T(1,128)S(1)} async-done(((f32[64,1,128]{2,1,0:T(1,128)}), f32[64,1,128]{2,1,0:T(1,128)S(1)}, u32[]{:S(2)}, u32[]{:S(2)}) %all-to-all-start.1) | async-done | bytes 32800 | tf_op jit(solution)/shard_map/all_to_all | solution.py:175
  73.2 0.1 reduce_sum.9
  73.3 0.6 broadcast_in_dim.10
  73.9 4.1 %all-to-all-start.2 = ((f32[12,1,128]{2,1,0:T(1,128)}), f32[12,1,128]{2,1,0:T(1,128)S(1)}, u32[]{:S(2)}, u32[]{:S(2)}) async-start(f32[12,1,128]{2,1,0:T(1,128)} %broadcast_in_dim.10), calls=%async_computation.2 | async-start | bytes 12288 | tf_op jit(solution)/shard_map/all_to_all | solution.py:177
  78.0 0.9 pad_maximum_fusion
  78.9 0.9 slice.39
  79.8 8.3 %all-to-all-done.2 = f32[12,1,128]{2,1,0:T(1,128)S(1)} async-done(((f32[12,1,128]{2,1,0:T(1,128)}), f32[12,1,128]{2,1,0:T(1,128)S(1)}, u32[]{:S(2)}, u32[]{:S(2)}) %all-to-all-start.2) | async-done | bytes 6176 | tf_op jit(solution)/shard_map/all_to_all | solution.py:177
  88.1 0.0 copy-done.3
  88.1 2.6 %update.1 = (f32[384,128]{1,0:T(8,128)}, f32[384,128]{1,0:T(8,128)}, bf16[400,128]{1,0:T(8,128)(2,1)S(1)}) custom-call(f32[12,128]{1,0:T(8,128)S(1)} %bitcast.51, f32[1,128]{1,0:T(1,128)S(1)} %pad_bitcast_fusion.lane_weight, f32[1]{0:T(128)S(6)} %add.63.phase, f32[8,4]{1,0:T(8,128)S(1)} %copy.25.first, f32[4]{0:T(128)S(1)} %copy-done.3, ...), custom_call_target="tpu_custom_call" | custom-call | tf_op jit(solution)/shard_map/update/pallas_call | solution.py:189
  90.7 28.7 %all-gather.2 = f16[4800,128]{1,0:T(8,128)(2,1)S(1)} all-gather(f16[400,128]{1,0:T(8,128)(2,1)S(1)} %convert_element_type.40), channel_id=2, replica_groups=mesh['hi'=4,'lo'=3,'mp_0'=4,'mp_1'=8,'mp_2'=2] {'hi','lo'}, dimensions={0}, use_global_device_ids=true | all-gather | bytes 1331200 | tf_op jit(solution)/shard_map/all_gather | solution.py:198
  119.4 0.3 fusion.3
  119.7 0.3 multiply_convert_fusion
  120.0 1.1 copy.27
  (7 shorter events, 0.1 us)
Async XLA Ops:
  2.1 23.7 %collective-permute-start = (bf16[2,4,192,128]{3,2,0,1:T(8,128)(2,1)S(1)}, bf16[2,4,192,128]{3,2,0,1:T(8,128)(2,1)S(1)}, u32[]{:S(2)}, u32[]{:S(2)}) collective-permute-start(bf16[2,4,192,128]{3,2,0,1:T(8,128)(2,1)S(1)} %bitcast.61), channel_id=1, source_target_pairs={{0,64},{64,128},{128,192},{192,256},{256,320},{320,384},{384,448},... | collective-permute-start | bytes 1179656 | tf_op jit(solution)/shard_map/ppermute | solution.py:37
  6.4 28.6 %copy-start.5 = (f32[10]{0:T(128)S(1)}, f32[10]{0:T(128)}, u32[]{:S(2)}) copy-start(f32[10]{0:T(128)} %param.17) | copy-start | bytes 124
  6.4 28.7 %copy-start.6 = (f32[4,2]{0,1:T(2,128)S(1)}, f32[4,2]{0,1:T(2,128)}, u32[]{:S(2)}) copy-start(f32[4,2]{0,1:T(2,128)} %param.16) | copy-start | bytes 100
  6.4 28.8 %copy-start.4 = (f32[8,4]{0,1:T(4,128)S(1)}, f32[8,4]{0,1:T(4,128)}, u32[]{:S(2)}) copy-start(f32[8,4]{0,1:T(4,128)} %param.14) | copy-start | bytes 388
  6.4 30.7 %copy-start = (f32[3,1,2,192,128]{4,3,2,1,0:T(8,128)S(1)}, f32[3,1,2,192,128]{4,3,2,1,0:T(8,128)}, u32[]{:S(2)}) copy-start(f32[3,1,2,192,128]{4,3,2,1,0:T(8,128)} %param.12) | copy-start | bytes 1769476
  6.4 20.7 %collective-permute-start.1 = (bf16[2,4,192,128]{3,2,0,1:T(8,128)(2,1)S(1)}, bf16[2,4,192,128]{3,2,0,1:T(8,128)(2,1)S(1)}, u32[]{:S(2)}, u32[]{:S(2)}) collective-permute-start(bf16[2,4,192,128]{3,2,0,1:T(8,128)(2,1)S(1)} %bitcast.62), channel_id=1, source_target_pairs={{0,704},{64,0},{128,64},{192,128},{256,192},{320,256},{384,320},{4... | collective-permute-start | bytes 1179656 | tf_op jit(solution)/shard_map/ppermute | solution.py:38
  28.0 24.6 %copy-start.1 = (f32[1,2,192,128]{3,2,1,0:T(8,128)S(1)}, f32[1,2,192,128]{3,2,1,0:T(8,128)}, u32[]{:S(2)}) copy-start(f32[1,2,192,128]{3,2,1,0:T(8,128)} %param.10) | copy-start | bytes 589828
  28.1 24.7 %copy-start.2 = (f32[3,1,2,192,128]{4,3,2,1,0:T(8,128)S(1)}, f32[3,1,2,192,128]{4,3,2,1,0:T(8,128)}, u32[]{:S(2)}) copy-start(f32[3,1,2,192,128]{4,3,2,1,0:T(8,128)} %param.11) | copy-start | bytes 1769476
  28.1 24.6 %all-to-all-start = ((bf16[4,2,192,128]{3,2,1,0:T(8,128)(2,1)}), bf16[4,2,192,128]{3,2,1,0:T(8,128)(2,1)S(1)}, u32[]{:S(2)}, u32[]{:S(2)}) async-start(bf16[4,2,192,128]{3,2,1,0:T(8,128)(2,1)} %fusion.2), calls=%async_computation | async-start | bytes 786432 | tf_op jit(solution)/shard_map/all_to_all | solution.py:41
  54.0 19.2 %all-to-all-start.1 = ((f32[64,1,128]{2,1,0:T(1,128)}), f32[64,1,128]{2,1,0:T(1,128)S(1)}, u32[]{:S(2)}, u32[]{:S(2)}) async-start(f32[64,1,128]{2,1,0:T(1,128)} %bitcast.10), calls=%async_computation.1 | async-start | bytes 65536 | tf_op jit(solution)/shard_map/all_to_all | solution.py:175
  65.7 22.4 %copy-start.3 = (f32[4]{0:T(128)S(1)}, f32[4]{0:T(128)}, u32[]{:S(2)}) copy-start(f32[4]{0:T(128)} %bias.1) | copy-start | bytes 52
  73.9 14.2 %all-to-all-start.2 = ((f32[12,1,128]{2,1,0:T(1,128)}), f32[12,1,128]{2,1,0:T(1,128)S(1)}, u32[]{:S(2)}, u32[]{:S(2)}) async-start(f32[12,1,128]{2,1,0:T(1,128)} %broadcast_in_dim.10), calls=%async_computation.2 | async-start | bytes 12288 | tf_op jit(solution)/shard_map/all_to_all | solution.py:177

commit v3 on v2

--- a/solution.py
+++ b/solution.py
@@ -10,6 +10,8 @@
 HQ = 4096
 DP = ("hi", "lo")
 MP = ("mp_0", "mp_1", "mp_2")
+PLANE = ("mp_0", "mp_1")
+COLUMN = ("hi", "lo", "mp_2")
 RATES = (0.9, 0.99, 0.999)
 FEATS = 8
 HIDDEN = 4
@@ -21,6 +23,7 @@
 
 VMEM = pl.BlockSpec(memory_space=pltpu.VMEM)
 SMEM = pl.BlockSpec(memory_space=pltpu.SMEM)
+HBM = pl.BlockSpec(memory_space=pltpu.HBM)
 PARAMS = pltpu.CompilerParams(vmem_limit_bytes=6 << 20)
 
 
@@ -82,7 +85,7 @@
 
 def update_kernel(
     totals, lane_weight, phase, first, bias, last, master, features,
-    update_out, master_out, params_out, scaled,
+    update_hbm, master_hbm, params_out, scaled, update_out, master_out, done,
 ):
     rows = master.shape[0]
     own = rows // NT
@@ -126,15 +129,19 @@
             return jnp.maximum(largest, jnp.max(jnp.abs(new).reshape(STEP // 8, 8, LANES), axis=0))
 
         largest = lax.fori_loop(0, own // STEP, body, largest)
+        half = pl.ds(t * own, own)
+        pltpu.make_async_copy(update_out.at[half], update_hbm.at[half], done.at[0, t]).start()
+        pltpu.make_async_copy(master_out.at[half], master_hbm.at[half], done.at[1, t]).start()
 
     most = jnp.max(jnp.max(largest, axis=0, keepdims=True), axis=1, keepdims=True) * 0.125
     power = jnp.full((1, 1), 0.125, jnp.float32)
-    grades = jnp.ones((1, LANES), jnp.float32)
+    grades = jnp.ones((TAIL, LANES), jnp.float32)
+    grade = lax.broadcasted_iota(jnp.int32, grades.shape, 0)
     for k in range(GRADES):
         small = most < 8.0
         most = jnp.where(small, most * 4096.0, most)
         power = jnp.where(small, power * 4096.0, power)
-        grades = jnp.where(jnp.logical_and(small, lane == k), 1.0 / 4096.0, grades)
+        grades = grades * jnp.where(grade == k, jnp.where(small, 1.0 / 4096.0, 1.0), 1.0)
     power = jnp.broadcast_to(power, (STEP, LANES))
 
     def write(i, carry):
@@ -144,14 +151,19 @@
         return carry
 
     lax.fori_loop(0, rows // STEP, write, 0)
-    params_out[rows:, :] = jnp.broadcast_to(grades, (TAIL, LANES)).astype(params_out.dtype)
+    params_out[rows:, :] = grades.astype(params_out.dtype)
+    for t in range(NT):
+        half = pl.ds(t * own, own)
+        pltpu.make_async_copy(update_out.at[half], update_hbm.at[half], done.at[0, t]).wait()
+        pltpu.make_async_copy(master_out.at[half], master_hbm.at[half], done.at[1, t]).wait()
 
 
 def local(
     grad_parts, master, momenta, second, step_count, mlp_first, mlp_bias, mlp_second, tensor_weight
 ):
     dp_count = lax.axis_size("hi") * lax.axis_size("lo")
-    mp_count = lax.axis_size("mp_0") * lax.axis_size("mp_1") * lax.axis_size("mp_2")
+    plane_count = lax.axis_size("mp_0") * lax.axis_size("mp_1")
+    column_count = dp_count * lax.axis_size("mp_2")
     _, nt, own, lanes = master.shape
     rows = nt * own
     f32, bf16 = jnp.float32, jnp.bfloat16
@@ -164,7 +176,7 @@
         moments_kernel,
         out_shape=(
             jax.ShapeDtypeStruct((FEATS - 1, rows, lanes), f32),
-            jax.ShapeDtypeStruct((mp_count, lanes), f32),
+            jax.ShapeDtypeStruct((plane_count, lanes), f32),
         ),
         in_specs=[VMEM] * 4,
         out_specs=(VMEM,) * 2,
@@ -172,9 +184,9 @@
         compiler_params=PARAMS,
         name="moments",
     )(got.reshape(-1, rows, lanes), old_master, momenta.reshape(3, rows, lanes), old_second)
-    sums = lax.all_to_all(sums, MP, 0, 0, tiled=True)
-    sums = jnp.broadcast_to(jnp.sum(sums, axis=0), (dp_count, lanes))
-    sums = lax.all_to_all(sums, DP, 0, 0, tiled=True)
+    sums = lax.all_to_all(sums, PLANE, 0, 0, tiled=True)
+    sums = jnp.broadcast_to(jnp.sum(sums, axis=0), (column_count, lanes))
+    sums = lax.all_to_all(sums, COLUMN, 0, 0, tiled=True)
 
     new_momenta = features[1:4]
     square = features[0] * features[0]
@@ -190,16 +202,24 @@
         update_kernel,
         out_shape=(state, state, jax.ShapeDtypeStruct((rows + TAIL, lanes), bf16)),
         in_specs=[VMEM, VMEM, SMEM, SMEM, SMEM, SMEM, VMEM, VMEM],
-        out_specs=(VMEM,) * 3,
-        scratch_shapes=[pltpu.VMEM((FEATS * HIDDEN, 8, LANES), f32)],
+        out_specs=(HBM, HBM, VMEM),
+        scratch_shapes=[
+            pltpu.VMEM((FEATS * HIDDEN, 8, LANES), f32),
+            pltpu.VMEM((rows, lanes), f32),
+            pltpu.VMEM((rows, lanes), f32),
+            pltpu.SemaphoreType.DMA((2, nt)),
+        ],
         compiler_params=PARAMS,
         name="update",
     )(sums, lane_weight, phase[None], mlp_first, mlp_bias, mlp_second, old_master, features)
     params = lax.all_gather(params.astype(jnp.float16), DP, axis=0, tiled=False)
-    scale = 8.0 * jnp.prod(params[:, rows, :GRADES].astype(f32), axis=1)
-    params = params[:, :rows].astype(f32) * scale[:, None, None]
-    params = params.astype(bf16).reshape(dp_count, nt, own, lanes)
-    new_params = jnp.moveaxis(params, 0, 1).reshape(1, nt, dp_count * own, lanes)
+    scale = 8.0 * jnp.prod(params[:, rows : rows + GRADES].astype(f32), axis=1, keepdims=True)
+    new_params = jnp.stack(
+        [
+            (params[:, t * own : (t + 1) * own].astype(f32) * scale).astype(bf16)
+            for t in range(nt)
+        ]
+    ).reshape(1, nt, dp_count * own, lanes)
     shape = master.shape
     return (
         new_params,

time: 122 us -> 120 us (0.984)
  the two profiles are of different devices: /device:TPU:2 before, /device:TPU:64 now
where the time goes in v3:
time: 120 us
  starting transfers between devices  39.5 us (33%)
  waiting for transfers between devices  35.7 us (30%)
  blocking collectives  29.4 us (24%)
  other arithmetic  5 us (4%)
  local copies, waits for them, and re-layouts  3.72 us (3%)
  Pallas kernels  3.64 us (3%)
  between operations  2.83 us (2%)
    all_gather x1, blocking collectives, local(): params = lax.all_gather(params.astype(jnp.float16), DP, axis=0, tiled=False)  29.4 us
    all_to_all x1, waiting for transfers between devices, reduced_gradient(): return lax.all_to_all(jnp.moveaxis(partial, 1, 0), 'hi', 0, 0, tiled=True)  14.8 us
    all_to_all x1, starting transfers between devices, reduced_gradient(): return lax.all_to_all(jnp.moveaxis(partial, 1, 0), 'hi', 0, 0, tiled=True)  13 us
    all_to_all x1, starting transfers between devices, local(): sums = lax.all_to_all(sums, PLANE, 0, 0, tiled=True)  9.95 us
    all_to_all x1, waiting for transfers between devices, local(): sums = lax.all_to_all(sums, PLANE, 0, 0, tiled=True)  8.74 us
    ppermute x1, starting transfers between devices, reduced_gradient(): lax.ppermute(of_class(lo_count - 1), DP, [(i, (i - 1) % count) for i in r...  8.19 us
    all_to_all x1, waiting for transfers between devices, local(): sums = lax.all_to_all(sums, COLUMN, 0, 0, tiled=True)  6.83 us
    ppermute x1, starting transfers between devices, reduced_gradient(): lax.ppermute(of_class(1), DP, [(i, (i + 1) % count) for i in range(count)])  4.28 us
  transfers between devices with their start and end apart: 5, of which 5 were waited for; matrix products, arithmetic and copies ran while one was open for 4% of the time, Pallas kernels for 0%

profile of v3, /device:TPU:64, one launch (start us, length us, event | category | flops | bytes accessed | tf_op | source)
XLA Modules:
  0.0 119.9 jit_solution(10222066231761764493)
XLA Ops:
  0.7 1.3 %constant_dynamic-slice_fusion.2 = (bf16[2,4,1,192,128]{4,3,2,1,0:T(8,128)(2,1)S(1)}, bf16[2,4,1,192,128]{4,3,2,1,0:T(8,128)(2,1)S(1)}, bf16[2,4,1,192,128]{4,3,2,1,0:T(8,128)(2,1)S(1)}) fusion(bf16[2,4,3,192,128]{4,3,2,1,0:T(8,128)(2,1)} %bitcast.52, s32[]{:T(128)S(6)} %select_n.26, s32[]{:T(128)S(6)} %select_n.30, s32[]{:T(128)S(6)} %select_n.28), kind=kLoop, calls=%fused_computation.22 | loop fusion | bytes 2359308 | tf_op jit(solution)/shard_map/jit(dynamic_index_in_dim)/dynamic_slice | solution.py:38
  2.1 4.3 %collective-permute-start = (bf16[2,4,192,128]{3,2,0,1:T(8,128)(2,1)S(1)}, bf16[2,4,192,128]{3,2,0,1:T(8,128)(2,1)S(1)}, u32[]{:S(2)}, u32[]{:S(2)}) collective-permute-start(bf16[2,4,192,128]{3,2,0,1:T(8,128)(2,1)S(1)} %bitcast.57), channel_id=1, source_target_pairs={{0,64},{64,128},{128,192},{192,256},{256,320},{320,384},{384,448},... | collective-permute-start | bytes 1179656 | tf_op jit(solution)/shard_map/ppermute | solution.py:40
  6.4 8.2 %collective-permute-start.1 = (bf16[2,4,192,128]{3,2,0,1:T(8,128)(2,1)S(1)}, bf16[2,4,192,128]{3,2,0,1:T(8,128)(2,1)S(1)}, u32[]{:S(2)}, u32[]{:S(2)}) collective-permute-start(bf16[2,4,192,128]{3,2,0,1:T(8,128)(2,1)S(1)} %bitcast.58), channel_id=1, source_target_pairs={{0,704},{64,0},{128,64},{192,128},{256,192},{320,256},{384,320},{4... | collective-permute-start | bytes 1179656 | tf_op jit(solution)/shard_map/ppermute | solution.py:41
  14.6 3.8 %collective-permute-done = bf16[2,4,192,128]{3,2,0,1:T(8,128)(2,1)S(1)} collective-permute-done((bf16[2,4,192,128]{3,2,0,1:T(8,128)(2,1)S(1)}, bf16[2,4,192,128]{3,2,0,1:T(8,128)(2,1)S(1)}, u32[]{:S(2)}, u32[]{:S(2)}) %collective-permute-start) | collective-permute-done | bytes 393248 | tf_op jit(solution)/shard_map/ppermute | solution.py:40
  18.4 1.5 %collective-permute-done.1 = bf16[2,4,192,128]{3,2,0,1:T(8,128)(2,1)S(1)} collective-permute-done((bf16[2,4,192,128]{3,2,0,1:T(8,128)(2,1)S(1)}, bf16[2,4,192,128]{3,2,0,1:T(8,128)(2,1)S(1)}, u32[]{:S(2)}, u32[]{:S(2)}) %collective-permute-start.1) | collective-permute-done | bytes 393248 | tf_op jit(solution)/shard_map/ppermute | solution.py:41
  19.8 0.0 copy-start.5
  19.9 0.0 copy-start.6
  19.9 0.0 copy-start.4
  19.9 0.0 copy-start
  19.9 0.9 fusion.2
  20.8 0.0 copy-start.1
  20.8 0.0 copy-start.2
  20.8 13.0 %all-to-all-start = ((bf16[4,2,192,128]{3,2,1,0:T(8,128)(2,1)}), bf16[4,2,192,128]{3,2,1,0:T(8,128)(2,1)S(1)}, u32[]{:S(2)}, u32[]{:S(2)}) async-start(bf16[4,2,192,128]{3,2,1,0:T(8,128)(2,1)} %fusion.2), calls=%async_computation | async-start | bytes 786432 | tf_op jit(solution)/shard_map/all_to_all | solution.py:44
  34.5 0.0 copy-done.5
  34.5 0.1 tile.10
  34.6 0.0 copy-done.6
  34.6 0.1 copy.25.last
  34.7 0.0 copy-done.4
  34.7 0.1 copy.24.first
  34.8 0.6 fusion.3
  36.7 0.0 copy-done
  36.7 0.7 slice_multiply_fusion.3
  37.4 14.8 %all-to-all-done = bf16[4,2,192,128]{3,2,1,0:T(8,128)(2,1)S(1)} async-done(((bf16[4,2,192,128]{3,2,1,0:T(8,128)(2,1)}), bf16[4,2,192,128]{3,2,1,0:T(8,128)(2,1)S(1)}, u32[]{:S(2)}, u32[]{:S(2)}) %all-to-all-start) | async-done | bytes 393248 | tf_op jit(solution)/shard_map/all_to_all | solution.py:44
  52.3 0.0 copy-done.1
  52.3 0.0 copy-done.2
  52.3 1.3 %moments.1 = (f32[7,384,128]{2,1,0:T(8,128)S(1)}, f32[32,128]{1,0:T(8,128)}) custom-call(bf16[4,384,128]{2,1,0:T(8,128)(2,1)S(1)} %bitcast.43, f32[384,128]{1,0:T(8,128)S(1)} %bitcast.44, f32[3,384,128]{2,1,0:T(8,128)S(1)} %bitcast.46, f32[3,384,128]{2,1,0:T(8,128)S(1)} %bitcast.42), custom_call_target="tpu_custom_call" | custom-call | tf_op jit(solution)/shard_map/moments/pallas_call | solution.py:175
  53.6 9.9 %all-to-all-start.1 = ((f32[32,1,128]{2,1,0:T(1,128)}), f32[32,1,128]{2,1,0:T(1,128)S(1)}, u32[]{:S(2)}, u32[]{:S(2)}) async-start(f32[32,1,128]{2,1,0:T(1,128)} %bitcast.10), calls=%async_computation.1 | async-start | bytes 32768 | tf_op jit(solution)/shard_map/all_to_all | solution.py:187
  63.5 1.0 bitcast_add_fusion.2
  64.5 8.7 %all-to-all-done.1 = f32[32,1,128]{2,1,0:T(1,128)S(1)} async-done(((f32[32,1,128]{2,1,0:T(1,128)}), f32[32,1,128]{2,1,0:T(1,128)S(1)}, u32[]{:S(2)}, u32[]{:S(2)}) %all-to-all-start.1) | async-done | bytes 16416 | tf_op jit(solution)/shard_map/all_to_all | solution.py:187
  73.3 0.1 reduce_sum.9
  73.3 0.6 broadcast_in_dim.10
  73.9 4.1 %all-to-all-start.2 = ((f32[24,1,128]{2,1,0:T(1,128)}), f32[24,1,128]{2,1,0:T(1,128)S(1)}, u32[]{:S(2)}, u32[]{:S(2)}) async-start(f32[24,1,128]{2,1,0:T(1,128)} %broadcast_in_dim.10), calls=%async_computation.2 | async-start | bytes 24576 | tf_op jit(solution)/shard_map/all_to_all | solution.py:189
  78.0 0.0 copy-start.3
  78.0 0.9 pad_maximum_fusion.1
  78.9 0.9 slice.43
  79.7 6.8 %all-to-all-done.2 = f32[24,1,128]{2,1,0:T(1,128)S(1)} async-done(((f32[24,1,128]{2,1,0:T(1,128)}), f32[24,1,128]{2,1,0:T(1,128)S(1)}, u32[]{:S(2)}, u32[]{:S(2)}) %all-to-all-start.2) | async-done | bytes 12320 | tf_op jit(solution)/shard_map/all_to_all | solution.py:189
  86.5 0.0 copy-done.3
  86.6 2.4 %update.1 = (f32[384,128]{1,0:T(8,128)}, f32[384,128]{1,0:T(8,128)}, bf16[400,128]{1,0:T(8,128)(2,1)S(1)}) custom-call(f32[24,128]{1,0:T(8,128)S(1)} %bitcast.47, f32[1,128]{1,0:T(1,128)S(1)} %pad_bitcast_fusion.lane_weight, f32[1]{0:T(128)S(6)} %add.63.phase, f32[8,4]{1,0:T(8,128)S(1)} %copy.24.first, f32[4]{0:T(128)S(1)} %copy-done.3, ...), custom_call_target="tpu_custom_call" | custom-call | tf_op jit(solution)/shard_map/update/pallas_call | solution.py:201
  88.9 29.4 %all-gather.2 = f16[4800,128]{1,0:T(8,128)(2,1)S(1)} all-gather(f16[400,128]{1,0:T(8,128)(2,1)S(1)} %convert_element_type.45), channel_id=2, replica_groups=mesh['hi'=4,'lo'=3,'mp_0'=4,'mp_1'=8,'mp_2'=2] {'hi','lo'}, dimensions={0}, use_global_device_ids=true | all-gather | bytes 1331200 | tf_op jit(solution)/shard_map/all_gather | solution.py:215
  118.4 0.3 multiply_convert_fusion.1
  118.7 1.1 pad_maximum_fusion
  (7 shorter events, 0.1 us)
Async XLA Ops:
  2.1 16.3 %collective-permute-start = (bf16[2,4,192,128]{3,2,0,1:T(8,128)(2,1)S(1)}, bf16[2,4,192,128]{3,2,0,1:T(8,128)(2,1)S(1)}, u32[]{:S(2)}, u32[]{:S(2)}) collective-permute-start(bf16[2,4,192,128]{3,2,0,1:T(8,128)(2,1)S(1)} %bitcast.57), channel_id=1, source_target_pairs={{0,64},{64,128},{128,192},{192,256},{256,320},{320,384},{384,448},... | collective-permute-start | bytes 1179656 | tf_op jit(solution)/shard_map/ppermute | solution.py:40
  6.4 13.5 %collective-permute-start.1 = (bf16[2,4,192,128]{3,2,0,1:T(8,128)(2,1)S(1)}, bf16[2,4,192,128]{3,2,0,1:T(8,128)(2,1)S(1)}, u32[]{:S(2)}, u32[]{:S(2)}) collective-permute-start(bf16[2,4,192,128]{3,2,0,1:T(8,128)(2,1)S(1)} %bitcast.58), channel_id=1, source_target_pairs={{0,704},{64,0},{128,64},{192,128},{256,192},{320,256},{384,320},{4... | collective-permute-start | bytes 1179656 | tf_op jit(solution)/shard_map/ppermute | solution.py:41
  19.8 14.7 %copy-start.5 = (f32[10]{0:T(128)S(1)}, f32[10]{0:T(128)}, u32[]{:S(2)}) copy-start(f32[10]{0:T(128)} %param.17) | copy-start | bytes 124
  19.9 14.8 %copy-start.6 = (f32[4,2]{0,1:T(2,128)S(1)}, f32[4,2]{0,1:T(2,128)}, u32[]{:S(2)}) copy-start(f32[4,2]{0,1:T(2,128)} %param.16) | copy-start | bytes 100
  19.9 14.9 %copy-start.4 = (f32[8,4]{0,1:T(4,128)S(1)}, f32[8,4]{0,1:T(4,128)}, u32[]{:S(2)}) copy-start(f32[8,4]{0,1:T(4,128)} %param.14) | copy-start | bytes 388
  19.9 16.8 %copy-start = (f32[3,1,2,192,128]{4,3,2,1,0:T(8,128)S(1)}, f32[3,1,2,192,128]{4,3,2,1,0:T(8,128)}, u32[]{:S(2)}) copy-start(f32[3,1,2,192,128]{4,3,2,1,0:T(8,128)} %param.12) | copy-start | bytes 1769476
  20.8 31.5 %copy-start.1 = (f32[1,2,192,128]{3,2,1,0:T(8,128)S(1)}, f32[1,2,192,128]{3,2,1,0:T(8,128)}, u32[]{:S(2)}) copy-start(f32[1,2,192,128]{3,2,1,0:T(8,128)} %param.10) | copy-start | bytes 589828
  20.8 31.5 %copy-start.2 = (f32[3,1,2,192,128]{4,3,2,1,0:T(8,128)S(1)}, f32[3,1,2,192,128]{4,3,2,1,0:T(8,128)}, u32[]{:S(2)}) copy-start(f32[3,1,2,192,128]{4,3,2,1,0:T(8,128)} %param.11) | copy-start | bytes 1769476
  20.8 31.5 %all-to-all-start = ((bf16[4,2,192,128]{3,2,1,0:T(8,128)(2,1)}), bf16[4,2,192,128]{3,2,1,0:T(8,128)(2,1)S(1)}, u32[]{:S(2)}, u32[]{:S(2)}) async-start(bf16[4,2,192,128]{3,2,1,0:T(8,128)(2,1)} %fusion.2), calls=%async_computation | async-start | bytes 786432 | tf_op jit(solution)/shard_map/all_to_all | solution.py:44
  53.6 19.7 %all-to-all-start.1 = ((f32[32,1,128]{2,1,0:T(1,128)}), f32[32,1,128]{2,1,0:T(1,128)S(1)}, u32[]{:S(2)}, u32[]{:S(2)}) async-start(f32[32,1,128]{2,1,0:T(1,128)} %bitcast.10), calls=%async_computation.1 | async-start | bytes 32768 | tf_op jit(solution)/shard_map/all_to_all | solution.py:187
  73.9 12.6 %all-to-all-start.2 = ((f32[24,1,128]{2,1,0:T(1,128)}), f32[24,1,128]{2,1,0:T(1,128)S(1)}, u32[]{:S(2)}, u32[]{:S(2)}) async-start(f32[24,1,128]{2,1,0:T(1,128)} %broadcast_in_dim.10), calls=%async_computation.2 | async-start | bytes 24576 | tf_op jit(solution)/shard_map/all_to_all | solution.py:189
  78.0 8.6 %copy-start.3 = (f32[4]{0:T(128)S(1)}, f32[4]{0:T(128)}, u32[]{:S(2)}) copy-start(f32[4]{0:T(128)} %bias.1) | copy-start | bytes 52

commit v4 on v3

--- a/solution.py
+++ b/solution.py
@@ -20,9 +20,12 @@
 STEP = 32
 TAIL = 16
 GRADES = 8
+BIAS = FEATS * HIDDEN
+LAST = BIAS + HIDDEN
+PHASE = LAST + 2 * HIDDEN
+LANE_WEIGHT = PHASE + 1
 
 VMEM = pl.BlockSpec(memory_space=pltpu.VMEM)
-SMEM = pl.BlockSpec(memory_space=pltpu.SMEM)
 HBM = pl.BlockSpec(memory_space=pltpu.HBM)
 PARAMS = pltpu.CompilerParams(vmem_limit_bytes=6 << 20)
 
@@ -84,7 +87,7 @@
 
 
 def update_kernel(
-    totals, lane_weight, phase, first, bias, last, master, features,
+    totals, weights, master, features,
     update_hbm, master_hbm, params_out, scaled, update_out, master_out, done,
 ):
     rows = master.shape[0]
@@ -92,22 +95,26 @@
     total = jnp.sum(totals[...], axis=0, keepdims=True)
     norms = jnp.sqrt(total / float(D * HQ) + 1e-06)
     inverse = 1.0 / norms
-    logs = lane_weight[...] * jnp.log(norms)
+    logs = weights[LANE_WEIGHT : LANE_WEIGHT + 1, :] * jnp.log(norms)
     lane = lax.broadcasted_iota(jnp.int32, logs.shape, 1)
 
     def rows_of(x):
         return jnp.broadcast_to(x[None], (STEP // 8, 8, LANES)).reshape(STEP, LANES)
+
+    def constant(k):
+        return jnp.broadcast_to(weights[k : k + 1, :], (STEP, LANES))
 
     largest = jnp.zeros((8, LANES), jnp.float32)
     for t in range(NT):
         mine = jnp.where(lane // FEATS == t, logs, 0.0)
-        logit = jnp.sum(mine, axis=1, keepdims=True) + phase[0]
+        logit = jnp.sum(mine, axis=1, keepdims=True) + weights[PHASE : PHASE + 1, 0:1]
         boost = rows_of(jnp.broadcast_to(jnp.exp(jnp.tanh(logit)), (8, LANES)))
         for f in range(FEATS):
             k = t * FEATS + f
             scale = jnp.broadcast_to(inverse[:, k : k + 1], (8, LANES))
             for j in range(HIDDEN):
-                scaled[f * HIDDEN + j] = first[f, j] * scale
+                k = f * HIDDEN + j
+                scaled[k] = weights[k : k + 1, :] * scale
 
         def body(i, largest):
             at = pl.ds(pl.multiple_of(t * own + i * STEP, STEP), STEP)
@@ -116,12 +123,12 @@
             direction = jnp.zeros((STEP, LANES), jnp.float32)
             magnitude = jnp.zeros((STEP, LANES), jnp.float32)
             for j in range(HIDDEN):
-                active = bias[j] + listing[0] * rows_of(scaled[j])
+                active = constant(BIAS + j) + listing[0] * rows_of(scaled[j])
                 for f in range(1, FEATS):
                     active = active + listing[f] * rows_of(scaled[f * HIDDEN + j])
                 active = jnp.maximum(active, 0.0)
-                direction = direction + last[j, 0] * active
-                magnitude = magnitude + last[j, 1] * active
+                direction = direction + constant(LAST + 2 * j) * active
+                magnitude = magnitude + constant(LAST + 2 * j + 1) * active
             step = direction * jnp.exp(0.5 * jnp.tanh(magnitude)) * boost
             new = old - 0.05 * step
             update_out[at, :] = step
@@ -198,10 +205,12 @@
     phase = tensor_weight[FEATS] * (jnp.log1p(step_value) / 11.5)
     phase = phase + tensor_weight[FEATS + 1] * (step_value / 100000.0)
     lane_weight = jnp.pad(jnp.tile(tensor_weight[:FEATS], nt), (0, lanes - nt * FEATS))[None]
+    flat = jnp.concatenate([mlp_first.reshape(-1), mlp_bias, mlp_second.reshape(-1), phase[None]])
+    weights = jnp.concatenate([jnp.broadcast_to(flat[:, None], (flat.shape[0], lanes)), lane_weight])
     update, new_master, params = pl.pallas_call(
         update_kernel,
         out_shape=(state, state, jax.ShapeDtypeStruct((rows + TAIL, lanes), bf16)),
-        in_specs=[VMEM, VMEM, SMEM, SMEM, SMEM, SMEM, VMEM, VMEM],
+        in_specs=[VMEM] * 4,
         out_specs=(HBM, HBM, VMEM),
         scratch_shapes=[
             pltpu.VMEM((FEATS * HIDDEN, 8, LANES), f32),
@@ -211,7 +220,7 @@
         ],
         compiler_params=PARAMS,
         name="update",
-    )(sums, lane_weight, phase[None], mlp_first, mlp_bias, mlp_second, old_master, features)
+    )(sums, weights, old_master, features)
     params = lax.all_gather(params.astype(jnp.float16), DP, axis=0, tiled=False)
     scale = 8.0 * jnp.prod(params[:, rows : rows + GRADES].astype(f32), axis=1, keepdims=True)
     new_params = jnp.stack(

time: 120 us -> 120 us (level)
  no operation moved by 1% of the time
where the time goes in v4:
time: 120 us; the launch traced here: 119 us
  starting transfers between devices  39.5 us (33%)
  waiting for transfers between devices  35.2 us (29%)
  blocking collectives  29.4 us (24%)
  other arithmetic  5.34 us (4%)
  local copies, waits for them, and re-layouts  3.89 us (3%)
  Pallas kernels  3.08 us (3%)
  between operations  2.83 us (2%)
    all_gather x1, blocking collectives, local(): params = lax.all_gather(params.astype(jnp.float16), DP, axis=0, tiled=False)  29.4 us
    all_to_all x1, waiting for transfers between devices, reduced_gradient(): return lax.all_to_all(jnp.moveaxis(partial, 1, 0), 'hi', 0, 0, tiled=True)  14.4 us
    all_to_all x1, starting transfers between devices, reduced_gradient(): return lax.all_to_all(jnp.moveaxis(partial, 1, 0), 'hi', 0, 0, tiled=True)  13.1 us
    all_to_all x1, starting transfers between devices, local(): sums = lax.all_to_all(sums, PLANE, 0, 0, tiled=True)  9.95 us
    all_to_all x1, waiting for transfers between devices, local(): sums = lax.all_to_all(sums, PLANE, 0, 0, tiled=True)  8.63 us
    ppermute x1, starting transfers between devices, reduced_gradient(): lax.ppermute(of_class(lo_count - 1), DP, [(i, (i - 1) % count) for i in r...  8.19 us
    all_to_all x1, waiting for transfers between devices, local(): sums = lax.all_to_all(sums, COLUMN, 0, 0, tiled=True)  6.84 us
    ppermute x1, starting transfers between devices, reduced_gradient(): lax.ppermute(of_class(1), DP, [(i, (i + 1) % count) for i in range(count)])  4.28 us
  transfers between devices with their start and end apart: 5, of which 5 were waited for; matrix products, arithmetic and copies ran while one was open for 4% of the time, Pallas kernels for 0%

profile of v4, /device:TPU:64, one launch (start us, length us, event | category | flops | bytes accessed | tf_op | source)
XLA Modules:
  0.0 119.3 jit_solution(12963837095969179454)
XLA Ops:
  0.7 1.3 %constant_dynamic-slice_fusion.2 = (bf16[2,4,1,192,128]{4,3,2,1,0:T(8,128)(2,1)S(1)}, bf16[2,4,1,192,128]{4,3,2,1,0:T(8,128)(2,1)S(1)}, bf16[2,4,1,192,128]{4,3,2,1,0:T(8,128)(2,1)S(1)}) fusion(bf16[2,4,3,192,128]{4,3,2,1,0:T(8,128)(2,1)} %bitcast.52, s32[]{:T(128)S(6)} %select_n.26, s32[]{:T(128)S(6)} %select_n.30, s32[]{:T(128)S(6)} %select_n.28), kind=kLoop, calls=%fused_computation.23 | loop fusion | bytes 2359308 | tf_op jit(solution)/shard_map/jit(dynamic_index_in_dim)/dynamic_slice | solution.py:41
  2.1 4.3 %collective-permute-start = (bf16[2,4,192,128]{3,2,0,1:T(8,128)(2,1)S(1)}, bf16[2,4,192,128]{3,2,0,1:T(8,128)(2,1)S(1)}, u32[]{:S(2)}, u32[]{:S(2)}) collective-permute-start(bf16[2,4,192,128]{3,2,0,1:T(8,128)(2,1)S(1)} %bitcast.57), channel_id=1, source_target_pairs={{0,64},{64,128},{128,192},{192,256},{256,320},{320,384},{384,448},... | collective-permute-start | bytes 1179656 | tf_op jit(solution)/shard_map/ppermute | solution.py:43
  6.4 8.2 %collective-permute-start.1 = (bf16[2,4,192,128]{3,2,0,1:T(8,128)(2,1)S(1)}, bf16[2,4,192,128]{3,2,0,1:T(8,128)(2,1)S(1)}, u32[]{:S(2)}, u32[]{:S(2)}) collective-permute-start(bf16[2,4,192,128]{3,2,0,1:T(8,128)(2,1)S(1)} %bitcast.58), channel_id=1, source_target_pairs={{0,704},{64,0},{128,64},{192,128},{256,192},{320,256},{384,320},{4... | collective-permute-start | bytes 1179656 | tf_op jit(solution)/shard_map/ppermute | solution.py:44
  14.6 3.8 %collective-permute-done = bf16[2,4,192,128]{3,2,0,1:T(8,128)(2,1)S(1)} collective-permute-done((bf16[2,4,192,128]{3,2,0,1:T(8,128)(2,1)S(1)}, bf16[2,4,192,128]{3,2,0,1:T(8,128)(2,1)S(1)}, u32[]{:S(2)}, u32[]{:S(2)}) %collective-permute-start) | collective-permute-done | bytes 393248 | tf_op jit(solution)/shard_map/ppermute | solution.py:43
  18.4 1.5 %collective-permute-done.1 = bf16[2,4,192,128]{3,2,0,1:T(8,128)(2,1)S(1)} collective-permute-done((bf16[2,4,192,128]{3,2,0,1:T(8,128)(2,1)S(1)}, bf16[2,4,192,128]{3,2,0,1:T(8,128)(2,1)S(1)}, u32[]{:S(2)}, u32[]{:S(2)}) %collective-permute-start.1) | collective-permute-done | bytes 393248 | tf_op jit(solution)/shard_map/ppermute | solution.py:44
  19.8 0.0 copy-start.4
  19.9 0.0 copy-start.5
  19.9 0.0 copy-start.3
  19.9 0.0 copy-start.6
  19.9 0.0 copy-start
  19.9 0.9 fusion.2
  20.8 0.0 copy-start.1
  20.8 0.0 copy-start.2
  20.8 13.1 %all-to-all-start = ((bf16[4,2,192,128]{3,2,1,0:T(8,128)(2,1)}), bf16[4,2,192,128]{3,2,1,0:T(8,128)(2,1)S(1)}, u32[]{:S(2)}, u32[]{:S(2)}) async-start(bf16[4,2,192,128]{3,2,1,0:T(8,128)(2,1)} %fusion.2), calls=%async_computation | async-start | bytes 786432 | tf_op jit(solution)/shard_map/all_to_all | solution.py:47
  34.5 0.0 copy-done.4
  34.5 0.1 tile.10
  34.6 0.0 copy-done.5
  34.6 0.1 copy.31
  34.7 0.1 reshape.115
  34.8 0.0 copy-done.3
  34.8 0.1 copy.30
  34.9 0.1 reshape.114
  35.0 0.6 fusion.3
  36.9 0.0 copy-done.6
  36.9 0.1 pad_maximum_fusion.3
  37.0 0.1 pad_maximum_fusion.2.weights
  37.0 0.0 copy-done
  37.0 0.8 slice_multiply_fusion.3
  37.8 14.4 %all-to-all-done = bf16[4,2,192,128]{3,2,1,0:T(8,128)(2,1)S(1)} async-done(((bf16[4,2,192,128]{3,2,1,0:T(8,128)(2,1)}), bf16[4,2,192,128]{3,2,1,0:T(8,128)(2,1)S(1)}, u32[]{:S(2)}, u32[]{:S(2)}) %all-to-all-start) | async-done | bytes 393248 | tf_op jit(solution)/shard_map/all_to_all | solution.py:47
  52.3 0.0 copy-done.1
  52.3 0.0 copy-done.2
  52.3 1.3 %moments.1 = (f32[7,384,128]{2,1,0:T(8,128)S(1)}, f32[32,128]{1,0:T(8,128)}) custom-call(bf16[4,384,128]{2,1,0:T(8,128)(2,1)S(1)} %bitcast.43, f32[384,128]{1,0:T(8,128)S(1)} %bitcast.44, f32[3,384,128]{2,1,0:T(8,128)S(1)} %bitcast.46, f32[3,384,128]{2,1,0:T(8,128)S(1)} %bitcast.42), custom_call_target="tpu_custom_call" | custom-call | tf_op jit(solution)/shard_map/moments/pallas_call | solution.py:182
  53.6 10.0 %all-to-all-start.1 = ((f32[32,1,128]{2,1,0:T(1,128)}), f32[32,1,128]{2,1,0:T(1,128)S(1)}, u32[]{:S(2)}, u32[]{:S(2)}) async-start(f32[32,1,128]{2,1,0:T(1,128)} %bitcast.10), calls=%async_computation.1 | async-start | bytes 32768 | tf_op jit(solution)/shard_map/all_to_all | solution.py:194
  63.5 1.1 bitcast_add_fusion.2
  64.6 8.6 %all-to-all-done.1 = f32[32,1,128]{2,1,0:T(1,128)S(1)} async-done(((f32[32,1,128]{2,1,0:T(1,128)}), f32[32,1,128]{2,1,0:T(1,128)S(1)}, u32[]{:S(2)}, u32[]{:S(2)}) %all-to-all-start.1) | async-done | bytes 16416 | tf_op jit(solution)/shard_map/all_to_all | solution.py:194
  73.3 0.1 reduce_sum.9
  73.3 0.6 broadcast_in_dim.16
  73.9 4.1 %all-to-all-start.2 = ((f32[24,1,128]{2,1,0:T(1,128)}), f32[24,1,128]{2,1,0:T(1,128)S(1)}, u32[]{:S(2)}, u32[]{:S(2)}) async-start(f32[24,1,128]{2,1,0:T(1,128)} %broadcast_in_dim.16), calls=%async_computation.2 | async-start | bytes 24576 | tf_op jit(solution)/shard_map/all_to_all | solution.py:196
  78.0 0.9 pad_maximum_fusion.1
  78.9 0.9 slice.43
  79.7 6.8 %all-to-all-done.2 = f32[24,1,128]{2,1,0:T(1,128)S(1)} async-done(((f32[24,1,128]{2,1,0:T(1,128)}), f32[24,1,128]{2,1,0:T(1,128)S(1)}, u32[]{:S(2)}, u32[]{:S(2)}) %all-to-all-start.2) | async-done | bytes 12320 | tf_op jit(solution)/shard_map/all_to_all | solution.py:196
  86.6 1.8 %update.1 = (f32[384,128]{1,0:T(8,128)}, f32[384,128]{1,0:T(8,128)}, bf16[400,128]{1,0:T(8,128)(2,1)S(1)}) custom-call(f32[24,128]{1,0:T(8,128)S(1)} %bitcast.47, f32[46,128]{1,0:T(8,128)S(1)} %pad_maximum_fusion.2.weights, f32[384,128]{1,0:T(8,128)S(1)} %bitcast.45, f32[7,384,128]{2,1,0:T(8,128)S(1)} %get-tuple-element.11.features), custom_call_target="tpu_custom_call" | custom-call | tf_op jit(solution)/shard_map/update/pallas_call | solution.py:210
  88.4 29.4 %all-gather.2 = f16[4800,128]{1,0:T(8,128)(2,1)S(1)} all-gather(f16[400,128]{1,0:T(8,128)(2,1)S(1)} %convert_element_type.45), channel_id=2, replica_groups=mesh['hi'=4,'lo'=3,'mp_0'=4,'mp_1'=8,'mp_2'=2] {'hi','lo'}, dimensions={0}, use_global_device_ids=true | all-gather | bytes 1331200 | tf_op jit(solution)/shard_map/all_gather | solution.py:224
  117.9 0.3 multiply_convert_fusion.1
  118.2 1.1 pad_maximum_fusion
  (7 shorter events, 0.1 us)
Async XLA Ops:
  2.1 16.3 %collective-permute-start = (bf16[2,4,192,128]{3,2,0,1:T(8,128)(2,1)S(1)}, bf16[2,4,192,128]{3,2,0,1:T(8,128)(2,1)S(1)}, u32[]{:S(2)}, u32[]{:S(2)}) collective-permute-start(bf16[2,4,192,128]{3,2,0,1:T(8,128)(2,1)S(1)} %bitcast.57), channel_id=1, source_target_pairs={{0,64},{64,128},{128,192},{192,256},{256,320},{320,384},{384,448},... | collective-permute-start | bytes 1179656 | tf_op jit(solution)/shard_map/ppermute | solution.py:43
  6.4 13.5 %collective-permute-start.1 = (bf16[2,4,192,128]{3,2,0,1:T(8,128)(2,1)S(1)}, bf16[2,4,192,128]{3,2,0,1:T(8,128)(2,1)S(1)}, u32[]{:S(2)}, u32[]{:S(2)}) collective-permute-start(bf16[2,4,192,128]{3,2,0,1:T(8,128)(2,1)S(1)} %bitcast.58), channel_id=1, source_target_pairs={{0,704},{64,0},{128,64},{192,128},{256,192},{320,256},{384,320},{4... | collective-permute-start | bytes 1179656 | tf_op jit(solution)/shard_map/ppermute | solution.py:44
  19.8 14.7 %copy-start.4 = (f32[10]{0:T(128)S(1)}, f32[10]{0:T(128)}, u32[]{:S(2)}) copy-start(f32[10]{0:T(128)} %param.17) | copy-start | bytes 124
  19.9 14.8 %copy-start.5 = (f32[4,2]{0,1:T(2,128)S(1)}, f32[4,2]{0,1:T(2,128)}, u32[]{:S(2)}) copy-start(f32[4,2]{0,1:T(2,128)} %param.16) | copy-start | bytes 100
  19.9 15.0 %copy-start.3 = (f32[8,4]{0,1:T(4,128)S(1)}, f32[8,4]{0,1:T(4,128)}, u32[]{:S(2)}) copy-start(f32[8,4]{0,1:T(4,128)} %param.14) | copy-start | bytes 388
  19.9 17.0 %copy-start.6 = (f32[4]{0:T(128)S(1)}, f32[4]{0:T(128)}, u32[]{:S(2)}) copy-start(f32[4]{0:T(128)} %param.15) | copy-start | bytes 52
  19.9 17.2 %copy-start = (f32[3,1,2,192,128]{4,3,2,1,0:T(8,128)S(1)}, f32[3,1,2,192,128]{4,3,2,1,0:T(8,128)}, u32[]{:S(2)}) copy-start(f32[3,1,2,192,128]{4,3,2,1,0:T(8,128)} %param.12) | copy-start | bytes 1769476
  20.8 31.5 %copy-start.1 = (f32[1,2,192,128]{3,2,1,0:T(8,128)S(1)}, f32[1,2,192,128]{3,2,1,0:T(8,128)}, u32[]{:S(2)}) copy-start(f32[1,2,192,128]{3,2,1,0:T(8,128)} %param.10) | copy-start | bytes 589828
  20.8 31.5 %copy-start.2 = (f32[3,1,2,192,128]{4,3,2,1,0:T(8,128)S(1)}, f32[3,1,2,192,128]{4,3,2,1,0:T(8,128)}, u32[]{:S(2)}) copy-start(f32[3,1,2,192,128]{4,3,2,1,0:T(8,128)} %param.11) | copy-start | bytes 1769476
  20.8 31.5 %all-to-all-start = ((bf16[4,2,192,128]{3,2,1,0:T(8,128)(2,1)}), bf16[4,2,192,128]{3,2,1,0:T(8,128)(2,1)S(1)}, u32[]{:S(2)}, u32[]{:S(2)}) async-start(bf16[4,2,192,128]{3,2,1,0:T(8,128)(2,1)} %fusion.2), calls=%async_computation | async-start | bytes 786432 | tf_op jit(solution)/shard_map/all_to_all | solution.py:47
  53.6 19.7 %all-to-all-start.1 = ((f32[32,1,128]{2,1,0:T(1,128)}), f32[32,1,128]{2,1,0:T(1,128)S(1)}, u32[]{:S(2)}, u32[]{:S(2)}) async-start(f32[32,1,128]{2,1,0:T(1,128)} %bitcast.10), calls=%async_computation.1 | async-start | bytes 32768 | tf_op jit(solution)/shard_map/all_to_all | solution.py:194
  73.9 12.6 %all-to-all-start.2 = ((f32[24,1,128]{2,1,0:T(1,128)}), f32[24,1,128]{2,1,0:T(1,128)S(1)}, u32[]{:S(2)}, u32[]{:S(2)}) async-start(f32[24,1,128]{2,1,0:T(1,128)} %broadcast_in_dim.16), calls=%async_computation.2 | async-start | bytes 24576 | tf_op jit(solution)/shard_map/all_to_all | solution.py:196

commit v5 on v4

--- a/solution.py
+++ b/solution.py
@@ -18,7 +18,7 @@
 NT = 2
 LANES = 128
 STEP = 32
-TAIL = 16
+TAIL = 8
 GRADES = 8
 BIAS = FEATS * HIDDEN
 LAST = BIAS + HIDDEN

time: 120 us -> 120 us (level)
  no operation moved by 1% of the time
where the time goes in v5:
time: 120 us; the launch traced here: 119 us
  starting transfers between devices  39.5 us (33%)
  waiting for transfers between devices  35.2 us (29%)
  blocking collectives  29.3 us (24%)
  other arithmetic  5.34 us (4%)
  local copies, waits for them, and re-layouts  3.89 us (3%)
  Pallas kernels  3.08 us (3%)
  between operations  2.83 us (2%)
    all_gather x1, blocking collectives, local(): params = lax.all_gather(params.astype(jnp.float16), DP, axis=0, tiled=False)  29.3 us
    all_to_all x1, waiting for transfers between devices, reduced_gradient(): return lax.all_to_all(jnp.moveaxis(partial, 1, 0), 'hi', 0, 0, tiled=True)  14.4 us
    all_to_all x1, starting transfers between devices, reduced_gradient(): return lax.all_to_all(jnp.moveaxis(partial, 1, 0), 'hi', 0, 0, tiled=True)  13.1 us
    all_to_all x1, starting transfers between devices, local(): sums = lax.all_to_all(sums, PLANE, 0, 0, tiled=True)  9.95 us
    all_to_all x1, waiting for transfers between devices, local(): sums = lax.all_to_all(sums, PLANE, 0, 0, tiled=True)  8.63 us
    ppermute x1, starting transfers between devices, reduced_gradient(): lax.ppermute(of_class(lo_count - 1), DP, [(i, (i - 1) % count) for i in r...  8.19 us
    all_to_all x1, waiting for transfers between devices, local(): sums = lax.all_to_all(sums, COLUMN, 0, 0, tiled=True)  6.84 us
    ppermute x1, starting transfers between devices, reduced_gradient(): lax.ppermute(of_class(1), DP, [(i, (i + 1) % count) for i in range(count)])  4.28 us
  transfers between devices with their start and end apart: 5, of which 5 were waited for; matrix products, arithmetic and copies ran while one was open for 4% of the time, Pallas kernels for 0%

profile of v5, /device:TPU:64, one launch (start us, length us, event | category | flops | bytes accessed | tf_op | source)
XLA Modules:
  0.0 119.2 jit_solution(13105103022406866965)
XLA Ops:
  0.7 1.3 %constant_dynamic-slice_fusion.2 = (bf16[2,4,1,192,128]{4,3,2,1,0:T(8,128)(2,1)S(1)}, bf16[2,4,1,192,128]{4,3,2,1,0:T(8,128)(2,1)S(1)}, bf16[2,4,1,192,128]{4,3,2,1,0:T(8,128)(2,1)S(1)}) fusion(bf16[2,4,3,192,128]{4,3,2,1,0:T(8,128)(2,1)} %bitcast.52, s32[]{:T(128)S(6)} %select_n.26, s32[]{:T(128)S(6)} %select_n.30, s32[]{:T(128)S(6)} %select_n.28), kind=kLoop, calls=%fused_computation.23 | loop fusion | bytes 2359308 | tf_op jit(solution)/shard_map/jit(dynamic_index_in_dim)/dynamic_slice | solution.py:41
  2.1 4.3 %collective-permute-start = (bf16[2,4,192,128]{3,2,0,1:T(8,128)(2,1)S(1)}, bf16[2,4,192,128]{3,2,0,1:T(8,128)(2,1)S(1)}, u32[]{:S(2)}, u32[]{:S(2)}) collective-permute-start(bf16[2,4,192,128]{3,2,0,1:T(8,128)(2,1)S(1)} %bitcast.57), channel_id=1, source_target_pairs={{0,64},{64,128},{128,192},{192,256},{256,320},{320,384},{384,448},... | collective-permute-start | bytes 1179656 | tf_op jit(solution)/shard_map/ppermute | solution.py:43
  6.4 8.2 %collective-permute-start.1 = (bf16[2,4,192,128]{3,2,0,1:T(8,128)(2,1)S(1)}, bf16[2,4,192,128]{3,2,0,1:T(8,128)(2,1)S(1)}, u32[]{:S(2)}, u32[]{:S(2)}) collective-permute-start(bf16[2,4,192,128]{3,2,0,1:T(8,128)(2,1)S(1)} %bitcast.58), channel_id=1, source_target_pairs={{0,704},{64,0},{128,64},{192,128},{256,192},{320,256},{384,320},{4... | collective-permute-start | bytes 1179656 | tf_op jit(solution)/shard_map/ppermute | solution.py:44
  14.6 3.8 %collective-permute-done = bf16[2,4,192,128]{3,2,0,1:T(8,128)(2,1)S(1)} collective-permute-done((bf16[2,4,192,128]{3,2,0,1:T(8,128)(2,1)S(1)}, bf16[2,4,192,128]{3,2,0,1:T(8,128)(2,1)S(1)}, u32[]{:S(2)}, u32[]{:S(2)}) %collective-permute-start) | collective-permute-done | bytes 393248 | tf_op jit(solution)/shard_map/ppermute | solution.py:43
  18.4 1.5 %collective-permute-done.1 = bf16[2,4,192,128]{3,2,0,1:T(8,128)(2,1)S(1)} collective-permute-done((bf16[2,4,192,128]{3,2,0,1:T(8,128)(2,1)S(1)}, bf16[2,4,192,128]{3,2,0,1:T(8,128)(2,1)S(1)}, u32[]{:S(2)}, u32[]{:S(2)}) %collective-permute-start.1) | collective-permute-done | bytes 393248 | tf_op jit(solution)/shard_map/ppermute | solution.py:44
  19.8 0.0 copy-start.4
  19.9 0.0 copy-start.5
  19.9 0.0 copy-start.3
  19.9 0.0 copy-start.6
  19.9 0.0 copy-start
  19.9 0.9 fusion.2
  20.8 0.0 copy-start.1
  20.8 0.0 copy-start.2
  20.8 13.1 %all-to-all-start = ((bf16[4,2,192,128]{3,2,1,0:T(8,128)(2,1)}), bf16[4,2,192,128]{3,2,1,0:T(8,128)(2,1)S(1)}, u32[]{:S(2)}, u32[]{:S(2)}) async-start(bf16[4,2,192,128]{3,2,1,0:T(8,128)(2,1)} %fusion.2), calls=%async_computation | async-start | bytes 786432 | tf_op jit(solution)/shard_map/all_to_all | solution.py:47
  34.5 0.0 copy-done.4
  34.5 0.1 tile.10
  34.6 0.0 copy-done.5
  34.6 0.1 copy.31
  34.7 0.1 reshape.115
  34.8 0.0 copy-done.3
  34.8 0.1 copy.30
  34.9 0.1 reshape.114
  35.0 0.6 fusion.3
  36.9 0.0 copy-done.6
  36.9 0.1 pad_maximum_fusion.3
  37.0 0.1 pad_maximum_fusion.2.weights
  37.0 0.0 copy-done
  37.0 0.8 slice_multiply_fusion.3
  37.8 14.4 %all-to-all-done = bf16[4,2,192,128]{3,2,1,0:T(8,128)(2,1)S(1)} async-done(((bf16[4,2,192,128]{3,2,1,0:T(8,128)(2,1)}), bf16[4,2,192,128]{3,2,1,0:T(8,128)(2,1)S(1)}, u32[]{:S(2)}, u32[]{:S(2)}) %all-to-all-start) | async-done | bytes 393248 | tf_op jit(solution)/shard_map/all_to_all | solution.py:47
  52.3 0.0 copy-done.1
  52.3 0.0 copy-done.2
  52.3 1.3 %moments.1 = (f32[7,384,128]{2,1,0:T(8,128)S(1)}, f32[32,128]{1,0:T(8,128)}) custom-call(bf16[4,384,128]{2,1,0:T(8,128)(2,1)S(1)} %bitcast.43, f32[384,128]{1,0:T(8,128)S(1)} %bitcast.44, f32[3,384,128]{2,1,0:T(8,128)S(1)} %bitcast.46, f32[3,384,128]{2,1,0:T(8,128)S(1)} %bitcast.42), custom_call_target="tpu_custom_call" | custom-call | tf_op jit(solution)/shard_map/moments/pallas_call | solution.py:182
  53.6 10.0 %all-to-all-start.1 = ((f32[32,1,128]{2,1,0:T(1,128)}), f32[32,1,128]{2,1,0:T(1,128)S(1)}, u32[]{:S(2)}, u32[]{:S(2)}) async-start(f32[32,1,128]{2,1,0:T(1,128)} %bitcast.10), calls=%async_computation.1 | async-start | bytes 32768 | tf_op jit(solution)/shard_map/all_to_all | solution.py:194
  63.5 1.1 bitcast_add_fusion.2
  64.6 8.6 %all-to-all-done.1 = f32[32,1,128]{2,1,0:T(1,128)S(1)} async-done(((f32[32,1,128]{2,1,0:T(1,128)}), f32[32,1,128]{2,1,0:T(1,128)S(1)}, u32[]{:S(2)}, u32[]{:S(2)}) %all-to-all-start.1) | async-done | bytes 16416 | tf_op jit(solution)/shard_map/all_to_all | solution.py:194
  73.3 0.1 reduce_sum.9
  73.3 0.6 broadcast_in_dim.16
  73.9 4.1 %all-to-all-start.2 = ((f32[24,1,128]{2,1,0:T(1,128)}), f32[24,1,128]{2,1,0:T(1,128)S(1)}, u32[]{:S(2)}, u32[]{:S(2)}) async-start(f32[24,1,128]{2,1,0:T(1,128)} %broadcast_in_dim.16), calls=%async_computation.2 | async-start | bytes 24576 | tf_op jit(solution)/shard_map/all_to_all | solution.py:196
  78.0 0.9 pad_maximum_fusion.1
  78.9 0.9 slice.43
  79.7 6.8 %all-to-all-done.2 = f32[24,1,128]{2,1,0:T(1,128)S(1)} async-done(((f32[24,1,128]{2,1,0:T(1,128)}), f32[24,1,128]{2,1,0:T(1,128)S(1)}, u32[]{:S(2)}, u32[]{:S(2)}) %all-to-all-start.2) | async-done | bytes 12320 | tf_op jit(solution)/shard_map/all_to_all | solution.py:196
  86.6 1.8 %update.1 = (f32[384,128]{1,0:T(8,128)}, f32[384,128]{1,0:T(8,128)}, bf16[392,128]{1,0:T(8,128)(2,1)S(1)}) custom-call(f32[24,128]{1,0:T(8,128)S(1)} %bitcast.47, f32[46,128]{1,0:T(8,128)S(1)} %pad_maximum_fusion.2.weights, f32[384,128]{1,0:T(8,128)S(1)} %bitcast.45, f32[7,384,128]{2,1,0:T(8,128)S(1)} %get-tuple-element.11.features), custom_call_target="tpu_custom_call" | custom-call | tf_op jit(solution)/shard_map/update/pallas_call | solution.py:210
  88.4 29.3 %all-gather.2 = f16[4704,128]{1,0:T(8,128)(2,1)S(1)} all-gather(f16[392,128]{1,0:T(8,128)(2,1)S(1)} %convert_element_type.45), channel_id=2, replica_groups=mesh['hi'=4,'lo'=3,'mp_0'=4,'mp_1'=8,'mp_2'=2] {'hi','lo'}, dimensions={0}, use_global_device_ids=true | all-gather | bytes 1304576 | tf_op jit(solution)/shard_map/all_gather | solution.py:224
  117.7 0.3 multiply_convert_fusion.1
  118.0 1.1 pad_maximum_fusion
  (7 shorter events, 0.1 us)
Async XLA Ops:
  2.1 16.3 %collective-permute-start = (bf16[2,4,192,128]{3,2,0,1:T(8,128)(2,1)S(1)}, bf16[2,4,192,128]{3,2,0,1:T(8,128)(2,1)S(1)}, u32[]{:S(2)}, u32[]{:S(2)}) collective-permute-start(bf16[2,4,192,128]{3,2,0,1:T(8,128)(2,1)S(1)} %bitcast.57), channel_id=1, source_target_pairs={{0,64},{64,128},{128,192},{192,256},{256,320},{320,384},{384,448},... | collective-permute-start | bytes 1179656 | tf_op jit(solution)/shard_map/ppermute | solution.py:43
  6.4 13.5 %collective-permute-start.1 = (bf16[2,4,192,128]{3,2,0,1:T(8,128)(2,1)S(1)}, bf16[2,4,192,128]{3,2,0,1:T(8,128)(2,1)S(1)}, u32[]{:S(2)}, u32[]{:S(2)}) collective-permute-start(bf16[2,4,192,128]{3,2,0,1:T(8,128)(2,1)S(1)} %bitcast.58), channel_id=1, source_target_pairs={{0,704},{64,0},{128,64},{192,128},{256,192},{320,256},{384,320},{4... | collective-permute-start | bytes 1179656 | tf_op jit(solution)/shard_map/ppermute | solution.py:44
  19.8 14.7 %copy-start.4 = (f32[10]{0:T(128)S(1)}, f32[10]{0:T(128)}, u32[]{:S(2)}) copy-start(f32[10]{0:T(128)} %param.17) | copy-start | bytes 124
  19.9 14.8 %copy-start.5 = (f32[4,2]{0,1:T(2,128)S(1)}, f32[4,2]{0,1:T(2,128)}, u32[]{:S(2)}) copy-start(f32[4,2]{0,1:T(2,128)} %param.16) | copy-start | bytes 100
  19.9 15.0 %copy-start.3 = (f32[8,4]{0,1:T(4,128)S(1)}, f32[8,4]{0,1:T(4,128)}, u32[]{:S(2)}) copy-start(f32[8,4]{0,1:T(4,128)} %param.14) | copy-start | bytes 388
  19.9 17.0 %copy-start.6 = (f32[4]{0:T(128)S(1)}, f32[4]{0:T(128)}, u32[]{:S(2)}) copy-start(f32[4]{0:T(128)} %param.15) | copy-start | bytes 52
  19.9 17.2 %copy-start = (f32[3,1,2,192,128]{4,3,2,1,0:T(8,128)S(1)}, f32[3,1,2,192,128]{4,3,2,1,0:T(8,128)}, u32[]{:S(2)}) copy-start(f32[3,1,2,192,128]{4,3,2,1,0:T(8,128)} %param.12) | copy-start | bytes 1769476
  20.8 31.5 %copy-start.1 = (f32[1,2,192,128]{3,2,1,0:T(8,128)S(1)}, f32[1,2,192,128]{3,2,1,0:T(8,128)}, u32[]{:S(2)}) copy-start(f32[1,2,192,128]{3,2,1,0:T(8,128)} %param.10) | copy-start | bytes 589828
  20.8 31.5 %copy-start.2 = (f32[3,1,2,192,128]{4,3,2,1,0:T(8,128)S(1)}, f32[3,1,2,192,128]{4,3,2,1,0:T(8,128)}, u32[]{:S(2)}) copy-start(f32[3,1,2,192,128]{4,3,2,1,0:T(8,128)} %param.11) | copy-start | bytes 1769476
  20.8 31.5 %all-to-all-start = ((bf16[4,2,192,128]{3,2,1,0:T(8,128)(2,1)}), bf16[4,2,192,128]{3,2,1,0:T(8,128)(2,1)S(1)}, u32[]{:S(2)}, u32[]{:S(2)}) async-start(bf16[4,2,192,128]{3,2,1,0:T(8,128)(2,1)} %fusion.2), calls=%async_computation | async-start | bytes 786432 | tf_op jit(solution)/shard_map/all_to_all | solution.py:47
  53.6 19.7 %all-to-all-start.1 = ((f32[32,1,128]{2,1,0:T(1,128)}), f32[32,1,128]{2,1,0:T(1,128)S(1)}, u32[]{:S(2)}, u32[]{:S(2)}) async-start(f32[32,1,128]{2,1,0:T(1,128)} %bitcast.10), calls=%async_computation.1 | async-start | bytes 32768 | tf_op jit(solution)/shard_map/all_to_all | solution.py:194
  73.9 12.6 %all-to-all-start.2 = ((f32[24,1,128]{2,1,0:T(1,128)}), f32[24,1,128]{2,1,0:T(1,128)S(1)}, u32[]{:S(2)}, u32[]{:S(2)}) async-start(f32[24,1,128]{2,1,0:T(1,128)} %broadcast_in_dim.16), calls=%async_computation.2 | async-start | bytes 24576 | tf_op jit(solution)/shard_map/all_to_all | solution.py:196

commit v6 on v5

--- a/solution.py
+++ b/solution.py
@@ -77,13 +77,16 @@
         for f in range(FEATS):
             k = t * FEATS + f
             table[k : k + 1, :] = jnp.sum(sums[f], axis=0, keepdims=True)
-    sums_out[...] = lax.dot_general(
-        jnp.ones(sums_out.shape, jnp.float32),
-        table[...],
-        (((1,), (1,)), ((), ())),
-        precision=lax.Precision.HIGHEST,
-        preferred_element_type=jnp.float32,
-    )
+    ones = jnp.ones((sums_out.shape[0], LANES), jnp.bfloat16)
+    left = table[...]
+    sums = jnp.zeros(sums_out.shape, jnp.float32)
+    for _ in range(3):
+        part = left.astype(jnp.bfloat16)
+        left = left - part.astype(jnp.float32)
+        sums = sums + lax.dot_general(
+            ones, part, (((1,), (1,)), ((), ())), preferred_element_type=jnp.float32
+        )
+    sums_out[...] = sums
 
 
 def update_kernel(

time: 120 us -> 120 us (level)
  no operation moved by 1% of the time
where the time goes in v6:
time: 120 us; the launch traced here: 119 us
  starting transfers between devices  39.5 us (33%)
  waiting for transfers between devices  35.2 us (29%)
  blocking collectives  29.3 us (24%)
  other arithmetic  5.34 us (4%)
  local copies, waits for them, and re-layouts  3.89 us (3%)
  Pallas kernels  3.04 us (3%)
  between operations  2.83 us (2%)
    all_gather x1, blocking collectives, local(): params = lax.all_gather(params.astype(jnp.float16), DP, axis=0, tiled=False)  29.3 us
    all_to_all x1, waiting for transfers between devices, reduced_gradient(): return lax.all_to_all(jnp.moveaxis(partial, 1, 0), 'hi', 0, 0, tiled=True)  14.4 us
    all_to_all x1, starting transfers between devices, reduced_gradient(): return lax.all_to_all(jnp.moveaxis(partial, 1, 0), 'hi', 0, 0, tiled=True)  13.1 us
    all_to_all x1, starting transfers between devices, local(): sums = lax.all_to_all(sums, PLANE, 0, 0, tiled=True)  9.95 us
    all_to_all x1, waiting for transfers between devices, local(): sums = lax.all_to_all(sums, PLANE, 0, 0, tiled=True)  8.63 us
    ppermute x1, starting transfers between devices, reduced_gradient(): lax.ppermute(of_class(lo_count - 1), DP, [(i, (i - 1) % count) for i in r...  8.19 us
    all_to_all x1, waiting for transfers between devices, local(): sums = lax.all_to_all(sums, COLUMN, 0, 0, tiled=True)  6.84 us
    ppermute x1, starting transfers between devices, reduced_gradient(): lax.ppermute(of_class(1), DP, [(i, (i + 1) % count) for i in range(count)])  4.28 us
  transfers between devices with their start and end apart: 5, of which 5 were waited for; matrix products, arithmetic and copies ran while one was open for 4% of the time, Pallas kernels for 0%

profile of v6, /device:TPU:64, one launch (start us, length us, event | category | flops | bytes accessed | tf_op | source)
XLA Modules:
  0.0 119.1 jit_solution(11765982272833447112)
XLA Ops:
  0.7 1.3 %constant_dynamic-slice_fusion.2 = (bf16[2,4,1,192,128]{4,3,2,1,0:T(8,128)(2,1)S(1)}, bf16[2,4,1,192,128]{4,3,2,1,0:T(8,128)(2,1)S(1)}, bf16[2,4,1,192,128]{4,3,2,1,0:T(8,128)(2,1)S(1)}) fusion(bf16[2,4,3,192,128]{4,3,2,1,0:T(8,128)(2,1)} %bitcast.52, s32[]{:T(128)S(6)} %select_n.26, s32[]{:T(128)S(6)} %select_n.30, s32[]{:T(128)S(6)} %select_n.28), kind=kLoop, calls=%fused_computation.23 | loop fusion | bytes 2359308 | tf_op jit(solution)/shard_map/jit(dynamic_index_in_dim)/dynamic_slice | solution.py:41
  2.1 4.3 %collective-permute-start = (bf16[2,4,192,128]{3,2,0,1:T(8,128)(2,1)S(1)}, bf16[2,4,192,128]{3,2,0,1:T(8,128)(2,1)S(1)}, u32[]{:S(2)}, u32[]{:S(2)}) collective-permute-start(bf16[2,4,192,128]{3,2,0,1:T(8,128)(2,1)S(1)} %bitcast.57), channel_id=1, source_target_pairs={{0,64},{64,128},{128,192},{192,256},{256,320},{320,384},{384,448},... | collective-permute-start | bytes 1179656 | tf_op jit(solution)/shard_map/ppermute | solution.py:43
  6.4 8.2 %collective-permute-start.1 = (bf16[2,4,192,128]{3,2,0,1:T(8,128)(2,1)S(1)}, bf16[2,4,192,128]{3,2,0,1:T(8,128)(2,1)S(1)}, u32[]{:S(2)}, u32[]{:S(2)}) collective-permute-start(bf16[2,4,192,128]{3,2,0,1:T(8,128)(2,1)S(1)} %bitcast.58), channel_id=1, source_target_pairs={{0,704},{64,0},{128,64},{192,128},{256,192},{320,256},{384,320},{4... | collective-permute-start | bytes 1179656 | tf_op jit(solution)/shard_map/ppermute | solution.py:44
  14.6 3.8 %collective-permute-done = bf16[2,4,192,128]{3,2,0,1:T(8,128)(2,1)S(1)} collective-permute-done((bf16[2,4,192,128]{3,2,0,1:T(8,128)(2,1)S(1)}, bf16[2,4,192,128]{3,2,0,1:T(8,128)(2,1)S(1)}, u32[]{:S(2)}, u32[]{:S(2)}) %collective-permute-start) | collective-permute-done | bytes 393248 | tf_op jit(solution)/shard_map/ppermute | solution.py:43
  18.4 1.5 %collective-permute-done.1 = bf16[2,4,192,128]{3,2,0,1:T(8,128)(2,1)S(1)} collective-permute-done((bf16[2,4,192,128]{3,2,0,1:T(8,128)(2,1)S(1)}, bf16[2,4,192,128]{3,2,0,1:T(8,128)(2,1)S(1)}, u32[]{:S(2)}, u32[]{:S(2)}) %collective-permute-start.1) | collective-permute-done | bytes 393248 | tf_op jit(solution)/shard_map/ppermute | solution.py:44
  19.8 0.0 copy-start.4
  19.9 0.0 copy-start.5
  19.9 0.0 copy-start.3
  19.9 0.0 copy-start.6
  19.9 0.0 copy-start
  19.9 0.9 fusion.2
  20.8 0.0 copy-start.1
  20.8 0.0 copy-start.2
  20.8 13.1 %all-to-all-start = ((bf16[4,2,192,128]{3,2,1,0:T(8,128)(2,1)}), bf16[4,2,192,128]{3,2,1,0:T(8,128)(2,1)S(1)}, u32[]{:S(2)}, u32[]{:S(2)}) async-start(bf16[4,2,192,128]{3,2,1,0:T(8,128)(2,1)} %fusion.2), calls=%async_computation | async-start | bytes 786432 | tf_op jit(solution)/shard_map/all_to_all | solution.py:47
  34.5 0.0 copy-done.4
  34.5 0.1 tile.10
  34.6 0.0 copy-done.5
  34.6 0.1 copy.31
  34.7 0.1 reshape.115
  34.8 0.0 copy-done.3
  34.8 0.1 copy.30
  34.9 0.1 reshape.114
  35.0 0.6 fusion.3
  36.9 0.0 copy-done.6
  36.9 0.1 pad_maximum_fusion.3
  37.0 0.1 pad_maximum_fusion.2.weights
  37.0 0.0 copy-done
  37.0 0.8 slice_multiply_fusion.3
  37.8 14.4 %all-to-all-done = bf16[4,2,192,128]{3,2,1,0:T(8,128)(2,1)S(1)} async-done(((bf16[4,2,192,128]{3,2,1,0:T(8,128)(2,1)}), bf16[4,2,192,128]{3,2,1,0:T(8,128)(2,1)S(1)}, u32[]{:S(2)}, u32[]{:S(2)}) %all-to-all-start) | async-done | bytes 393248 | tf_op jit(solution)/shard_map/all_to_all | solution.py:47
  52.3 0.0 copy-done.1
  52.3 0.0 copy-done.2
  52.3 1.2 %moments.1 = (f32[7,384,128]{2,1,0:T(8,128)S(1)}, f32[32,128]{1,0:T(8,128)}) custom-call(bf16[4,384,128]{2,1,0:T(8,128)(2,1)S(1)} %bitcast.43, f32[384,128]{1,0:T(8,128)S(1)} %bitcast.44, f32[3,384,128]{2,1,0:T(8,128)S(1)} %bitcast.46, f32[3,384,128]{2,1,0:T(8,128)S(1)} %bitcast.42), custom_call_target="tpu_custom_call" | custom-call | tf_op jit(solution)/shard_map/moments/pallas_call | solution.py:185
  53.5 10.0 %all-to-all-start.1 = ((f32[32,1,128]{2,1,0:T(1,128)}), f32[32,1,128]{2,1,0:T(1,128)S(1)}, u32[]{:S(2)}, u32[]{:S(2)}) async-start(f32[32,1,128]{2,1,0:T(1,128)} %bitcast.10), calls=%async_computation.1 | async-start | bytes 32768 | tf_op jit(solution)/shard_map/all_to_all | solution.py:197
  63.5 1.1 bitcast_add_fusion.2
  64.6 8.6 %all-to-all-done.1 = f32[32,1,128]{2,1,0:T(1,128)S(1)} async-done(((f32[32,1,128]{2,1,0:T(1,128)}), f32[32,1,128]{2,1,0:T(1,128)S(1)}, u32[]{:S(2)}, u32[]{:S(2)}) %all-to-all-start.1) | async-done | bytes 16416 | tf_op jit(solution)/shard_map/all_to_all | solution.py:197
  73.2 0.1 reduce_sum.9
  73.3 0.6 broadcast_in_dim.16
  73.9 4.1 %all-to-all-start.2 = ((f32[24,1,128]{2,1,0:T(1,128)}), f32[24,1,128]{2,1,0:T(1,128)S(1)}, u32[]{:S(2)}, u32[]{:S(2)}) async-start(f32[24,1,128]{2,1,0:T(1,128)} %broadcast_in_dim.16), calls=%async_computation.2 | async-start | bytes 24576 | tf_op jit(solution)/shard_map/all_to_all | solution.py:199
  78.0 0.9 pad_maximum_fusion.1
  78.8 0.9 slice.43
  79.7 6.8 %all-to-all-done.2 = f32[24,1,128]{2,1,0:T(1,128)S(1)} async-done(((f32[24,1,128]{2,1,0:T(1,128)}), f32[24,1,128]{2,1,0:T(1,128)S(1)}, u32[]{:S(2)}, u32[]{:S(2)}) %all-to-all-start.2) | async-done | bytes 12320 | tf_op jit(solution)/shard_map/all_to_all | solution.py:199
  86.5 1.8 %update.1 = (f32[384,128]{1,0:T(8,128)}, f32[384,128]{1,0:T(8,128)}, bf16[392,128]{1,0:T(8,128)(2,1)S(1)}) custom-call(f32[24,128]{1,0:T(8,128)S(1)} %bitcast.47, f32[46,128]{1,0:T(8,128)S(1)} %pad_maximum_fusion.2.weights, f32[384,128]{1,0:T(8,128)S(1)} %bitcast.45, f32[7,384,128]{2,1,0:T(8,128)S(1)} %get-tuple-element.11.features), custom_call_target="tpu_custom_call" | custom-call | tf_op jit(solution)/shard_map/update/pallas_call | solution.py:213
  88.4 29.3 %all-gather.2 = f16[4704,128]{1,0:T(8,128)(2,1)S(1)} all-gather(f16[392,128]{1,0:T(8,128)(2,1)S(1)} %convert_element_type.45), channel_id=2, replica_groups=mesh['hi'=4,'lo'=3,'mp_0'=4,'mp_1'=8,'mp_2'=2] {'hi','lo'}, dimensions={0}, use_global_device_ids=true | all-gather | bytes 1304576 | tf_op jit(solution)/shard_map/all_gather | solution.py:227
  117.7 0.3 multiply_convert_fusion.1
  118.0 1.1 pad_maximum_fusion
  (7 shorter events, 0.1 us)
Async XLA Ops:
  2.1 16.3 %collective-permute-start = (bf16[2,4,192,128]{3,2,0,1:T(8,128)(2,1)S(1)}, bf16[2,4,192,128]{3,2,0,1:T(8,128)(2,1)S(1)}, u32[]{:S(2)}, u32[]{:S(2)}) collective-permute-start(bf16[2,4,192,128]{3,2,0,1:T(8,128)(2,1)S(1)} %bitcast.57), channel_id=1, source_target_pairs={{0,64},{64,128},{128,192},{192,256},{256,320},{320,384},{384,448},... | collective-permute-start | bytes 1179656 | tf_op jit(solution)/shard_map/ppermute | solution.py:43
  6.4 13.5 %collective-permute-start.1 = (bf16[2,4,192,128]{3,2,0,1:T(8,128)(2,1)S(1)}, bf16[2,4,192,128]{3,2,0,1:T(8,128)(2,1)S(1)}, u32[]{:S(2)}, u32[]{:S(2)}) collective-permute-start(bf16[2,4,192,128]{3,2,0,1:T(8,128)(2,1)S(1)} %bitcast.58), channel_id=1, source_target_pairs={{0,704},{64,0},{128,64},{192,128},{256,192},{320,256},{384,320},{4... | collective-permute-start | bytes 1179656 | tf_op jit(solution)/shard_map/ppermute | solution.py:44
  19.8 14.7 %copy-start.4 = (f32[10]{0:T(128)S(1)}, f32[10]{0:T(128)}, u32[]{:S(2)}) copy-start(f32[10]{0:T(128)} %param.17) | copy-start | bytes 124
  19.9 14.8 %copy-start.5 = (f32[4,2]{0,1:T(2,128)S(1)}, f32[4,2]{0,1:T(2,128)}, u32[]{:S(2)}) copy-start(f32[4,2]{0,1:T(2,128)} %param.16) | copy-start | bytes 100
  19.9 15.0 %copy-start.3 = (f32[8,4]{0,1:T(4,128)S(1)}, f32[8,4]{0,1:T(4,128)}, u32[]{:S(2)}) copy-start(f32[8,4]{0,1:T(4,128)} %param.14) | copy-start | bytes 388
  19.9 17.0 %copy-start.6 = (f32[4]{0:T(128)S(1)}, f32[4]{0:T(128)}, u32[]{:S(2)}) copy-start(f32[4]{0:T(128)} %param.15) | copy-start | bytes 52
  19.9 17.2 %copy-start = (f32[3,1,2,192,128]{4,3,2,1,0:T(8,128)S(1)}, f32[3,1,2,192,128]{4,3,2,1,0:T(8,128)}, u32[]{:S(2)}) copy-start(f32[3,1,2,192,128]{4,3,2,1,0:T(8,128)} %param.12) | copy-start | bytes 1769476
  20.8 31.5 %copy-start.1 = (f32[1,2,192,128]{3,2,1,0:T(8,128)S(1)}, f32[1,2,192,128]{3,2,1,0:T(8,128)}, u32[]{:S(2)}) copy-start(f32[1,2,192,128]{3,2,1,0:T(8,128)} %param.10) | copy-start | bytes 589828
  20.8 31.5 %copy-start.2 = (f32[3,1,2,192,128]{4,3,2,1,0:T(8,128)S(1)}, f32[3,1,2,192,128]{4,3,2,1,0:T(8,128)}, u32[]{:S(2)}) copy-start(f32[3,1,2,192,128]{4,3,2,1,0:T(8,128)} %param.11) | copy-start | bytes 1769476
  20.8 31.5 %all-to-all-start = ((bf16[4,2,192,128]{3,2,1,0:T(8,128)(2,1)}), bf16[4,2,192,128]{3,2,1,0:T(8,128)(2,1)S(1)}, u32[]{:S(2)}, u32[]{:S(2)}) async-start(bf16[4,2,192,128]{3,2,1,0:T(8,128)(2,1)} %fusion.2), calls=%async_computation | async-start | bytes 786432 | tf_op jit(solution)/shard_map/all_to_all | solution.py:47
  53.5 19.7 %all-to-all-start.1 = ((f32[32,1,128]{2,1,0:T(1,128)}), f32[32,1,128]{2,1,0:T(1,128)S(1)}, u32[]{:S(2)}, u32[]{:S(2)}) async-start(f32[32,1,128]{2,1,0:T(1,128)} %bitcast.10), calls=%async_computation.1 | async-start | bytes 32768 | tf_op jit(solution)/shard_map/all_to_all | solution.py:197
  73.9 12.6 %all-to-all-start.2 = ((f32[24,1,128]{2,1,0:T(1,128)}), f32[24,1,128]{2,1,0:T(1,128)S(1)}, u32[]{:S(2)}, u32[]{:S(2)}) async-start(f32[24,1,128]{2,1,0:T(1,128)} %broadcast_in_dim.16), calls=%async_computation.2 | async-start | bytes 24576 | tf_op jit(solution)/shard_map/all_to_all | solution.py:199
